TPU v7x, 32 devices: a whole 2x2x4 slice. The times are simulated.
32 devices in a mesh: section: 4 (over z), shard: 8 (over y, x, core).
Axes of the slice: x: 2, y: 2, z: 4, core: 2. Of those that a mesh axis runs over, the one named last changes fastest.
Arguments:
- grad_parts: bfloat16 [4, 8, 256, 8192], P('section', 'shard'), may hold values from -6 to 6
- params: bfloat16 [4, 256, 8192], P('section', 'shard'), may hold values from -6 to 6
- moment_first: float32 [4, 256, 8192], P('section', 'shard'), may hold values from -6 to 6
- moment_second: float32 [4, 256, 8192], P('section', 'shard'), may hold values from 0.5 to 50
- block_layer: int32 [4, 32], P('section', 'shard'), may hold values from 0 to 7, as said below
- block_valid: int32 [4, 32], P('section', 'shard'), may hold values from 0 to 1
- decay: float32 [8], replicated, may hold values from 0.05 to 1
Outputs:
- new_params: bfloat16 [4, 256, 8192], P('section', 'shard')
- new_first: float32 [4, 256, 8192], P('section', 'shard')
- new_second: float32 [4, 256, 8192], P('section', 'shard')
- ratios: float32 [8], replicated
Inputs may be any that keep to these rules, and one draw needn't show every extreme that they name: `block_layer`: in every section the live slots come first. One section has all 32 slots live; each other section has between 16 and 32 live slots, and all sections together have 3 * 32. Over the live slots taken section by section in order, layer ids never fall and every layer has exactly 12 live slots; dead slots hold arbitrary layer ids.
All inputs are finite; a program needn't handle non-finite values.
Results may differ from a plain program's by a relative error of at most 0.008.
Values may be sent and summed in bfloat16 or wider, within the bound.
A program may use at most 64 MiB of HBM per device.

v0:
```python
import functools
import math

import jax
import jax.numpy as jnp
from jax import lax
from jax.experimental import pallas as pl
from jax.experimental.pallas import tpu as pltpu
from jax.sharding import PartitionSpec as P

MESH = pl.DeviceIdType.MESH
bias_first = 1.0 - 0.9**10
bias_second = 1.0 - 0.99**10
LANES = 128
PIECES = 8
ONE_SHOT = True
PARTS = 2


def kernel(
    n_sec, n_y, n_x, pieces,
    g_hbm, p_hbm, m1_hbm, m2_hbm, layer_ref, valid_ref, decay_ref,
    p_v, upd, new1_ref, new2_ref, step_ref, ratio_ref,
    own, away, d2d, m1_v, m2_v, r1a, r1b, s1a, s1b, r2a, r2b, tiles, ztiles,
    load_sem, state_sem, pair_sem, one_send, one_recv, two_send, two_recv,
    t_send, t_recv, z_send, z_recv, told, xa, xb, raw_send, raw_recv,
):
    rows, cols = p_v.shape
    width = cols // pieces
    raw = xa.shape[-1]
    n_shard = 2 * n_y * n_x
    sec, me = lax.axis_index("section"), lax.axis_index("shard")
    core = lax.rem(me, 2)
    x = lax.rem(me // 2, n_x)
    y = me // (2 * n_x)
    blocks = layer_ref.shape[1]
    block_rows = rows // blocks

    def at(yy, xx, cc):
        return (sec, (yy * n_x + xx) * 2 + cc)

    def span(p):
        return pl.ds(p * width, width)

    loads = []
    for p in range(pieces):
        a = pltpu.make_async_copy(g_hbm.at[:, :, 1 - core, :, span(p)], away.at[:, :, :, span(p)], load_sem.at[0, p])
        b = pltpu.make_async_copy(g_hbm.at[:, :, core, :, span(p)], own.at[:, :, :, span(p)], load_sem.at[1, p])
        a.start()
        b.start()
        loads.append((a, b))
    states = [
        pltpu.make_async_copy(src, dst, state_sem.at[i])
        for i, (src, dst) in enumerate(((p_hbm, p_v), (m1_hbm, m1_v), (m2_hbm, m2_v)))
    ]
    for s in states:
        s.start()

    barrier = pltpu.get_barrier_semaphore()
    near = [at(y, x, 1 - core)]
    for cc in (core, 1 - core):
        near += [at(y, lax.rem(x + j, n_x), cc) for j in range(1, n_x)]
        near += [at(lax.rem(y + j, n_y), x, cc) for j in range(1, n_y)]
    for peer in near:
        pl.semaphore_signal(barrier, inc=1, device_id=peer, device_id_type=MESH)
    last_sec = n_sec - 1
    up = (jnp.minimum(sec + 1, last_sec), me)
    down = (jnp.maximum(sec - 1, 0), me)

    @pl.when(sec < last_sec)
    def _():
        pl.semaphore_signal(barrier, inc=1, device_id=up, device_id_type=MESH)

    @pl.when(sec > 0)
    def _():
        pl.semaphore_signal(barrier, inc=1, device_id=down, device_id_type=MESH)

    ends = jnp.where(sec < last_sec, 1, 0) + jnp.where(sec > 0, 1, 0)
    pl.semaphore_wait(barrier, len(near) + ends)

    def relay(d):
        if d > 1:

            @pl.when(sec >= d - 1)
            def _():
                pl.semaphore_wait(told.at[0, d - 2], 1)

            @pl.when(sec <= n_sec - d)
            def _():
                pl.semaphore_wait(told.at[1, d - 2], 1)

        if d < n_sec:

            @pl.when((sec >= d - 1) & (sec < last_sec))
            def _():
                pl.semaphore_signal(told.at[0, d - 1], inc=1, device_id=up, device_id_type=MESH)

            @pl.when((sec <= n_sec - d) & (sec > 0))
            def _():
                pl.semaphore_signal(told.at[1, d - 1], inc=1, device_id=down, device_id_type=MESH)

    def raw_span(p):
        return pl.ds(p * width, raw)

    def send_raw(p):
        loads[p][1].wait()
        group = []
        for j in range(1, n_y if p else n_x):
            for which, (buffer, cc) in enumerate(((own, core), (away, 1 - core))):
                if p == 0:
                    t = lax.rem(x + j, n_x)
                    src, dev = buffer.at[:, t, :, raw_span(p)], at(y, t, cc)
                else:
                    t = lax.rem(y + j, n_y)
                    src, dev = buffer.at[t, :, :, raw_span(p)], at(t, x, cc)
                first_dst, other_dst = (r1b, xb) if p else (r1a, xa)
                c = pltpu.make_async_remote_copy(
                    src_ref=src,
                    dst_ref=other_dst.at[j - 1] if which else first_dst.at[0, j - 1, :, :, pl.ds(0, raw)],
                    send_sem=raw_send.at[p, which, j - 1], recv_sem=raw_recv.at[p, which, j - 1],
                    device_id=dev, device_id_type=MESH,
                )
                c.start()
                group.append(c)
        return group

    pair = []
    for p in range(pieces):
        loads[p][0].wait()
        c = pltpu.make_async_remote_copy(
            src_ref=away.at[:, :, :, span(p)], dst_ref=d2d.at[:, :, :, span(p)],
            send_sem=pair_sem.at[0, p], recv_sem=pair_sem.at[1, p],
            device_id=at(y, x, 1 - core), device_id_type=MESH,
        )
        c.start()
        pair.append(c)
        if p == 1:
            raws = [send_raw(0), send_raw(1)]

    ones = []
    for p in range(pieces):
        if p > 1:
            loads[p][1].wait()
        pair[p].wait_recv()
        along_x = p % 2 == 0
        skip = raw if p < 2 else 0
        rest = pl.ds(p * width + skip, width - skip)

        def add_pair(yy, xx, cut):
            total = own[yy, xx, :, cut].astype(jnp.float32) + d2d[yy, xx, :, cut].astype(jnp.float32)
            own[yy, xx, :, cut] = total.astype(jnp.bfloat16)

        def add_all(i, carry, rest=rest):
            add_pair(i // n_x, lax.rem(i, n_x), rest)
            return carry

        lax.fori_loop(0, n_y * n_x, add_all, 0)
        group = []
        for j in range(1, n_x if along_x else n_y):
            landing = pl.ds(skip, width - skip)
            if along_x:
                t = lax.rem(x + j, n_x)
                src, dev = own.at[:, t, :, rest], at(y, t, core)
                dst = r1a.at[p // 2, j - 1, :, :, landing]
            else:
                t = lax.rem(y + j, n_y)
                src, dev = own.at[t, :, :, rest], at(t, x, core)
                dst = r1b.at[p // 2, j - 1, :, :, landing]
            c = pltpu.make_async_remote_copy(
                src_ref=src, dst_ref=dst,
                send_sem=one_send.at[p, j - 1], recv_sem=one_recv.at[p, j - 1],
                device_id=dev, device_id_type=MESH,
            )
            c.start()
            group.append(c)
        ones.append(group)
        if p < 2:
            for i in range(n_y if along_x else n_x):
                add_pair(i if along_x else y, x if along_x else i, raw_span(p))

    twos = []
    for p in range(pieces):
        for c in ones[p]:
            c.wait_recv()
        if p < 2:
            for c in raws[p]:
                c.wait_recv()
            for k in range(n_y - 1 if p else n_x - 1):
                landed, other = (r1b, xb) if p else (r1a, xa)
                total = landed[0, k, :, :, :raw].astype(jnp.float32) + other[k].astype(jnp.float32)
                landed[0, k, :, :, :raw] = total.astype(jnp.bfloat16)
        group = []
        along_x = p % 2 == 0
        for j in range(1, n_y if along_x else n_x):
            if along_x:
                t = lax.rem(y + j, n_y)
                total = own[t, x, :, span(p)].astype(jnp.float32)
                for k in range(n_x - 1):
                    total += r1a[p // 2, k, t].astype(jnp.float32)
                s1a[p // 2, j - 1] = total.astype(jnp.bfloat16)
                src, dst, dev = s1a.at[p // 2, j - 1], r2a.at[p // 2, j - 1], at(t, x, core)
            else:
                t = lax.rem(x + j, n_x)
                total = own[y, t, :, span(p)].astype(jnp.float32)
                for k in range(n_y - 1):
                    total += r1b[p // 2, k, t].astype(jnp.float32)
                s1b[p // 2, j - 1] = total.astype(jnp.bfloat16)
                src, dst, dev = s1b.at[p // 2, j - 1], r2b.at[p // 2, j - 1], at(y, t, core)
            c = pltpu.make_async_remote_copy(
                src_ref=src, dst_ref=dst,
                send_sem=two_send.at[p, j - 1], recv_sem=two_recv.at[p, j - 1],
                device_id=dev, device_id_type=MESH,
            )
            c.start()
            group.append(c)
        twos.append(group)

    def by_block(scalars):
        return jnp.concatenate([jnp.full((block_rows, LANES), s) for s in scalars], axis=0)

    layers = [layer_ref[0, b] for b in range(blocks)]
    lives = [valid_ref[0, b] for b in range(blocks)]
    row_decay = by_block([decay_ref[layer] for layer in layers])
    row_live = by_block([jnp.where(v > 0, 1.0, 0.0).astype(jnp.float32) for v in lives]) > 0.5

    for s in states:
        s.wait()

    zero = jnp.zeros((rows, LANES), jnp.float32)
    sums = (zero, zero)
    for p in range(pieces):
        for c in twos[p]:
            c.wait_recv()
        along_x = p % 2 == 0

        def update_piece(i, sums, p=p, along_x=along_x):
            usum, wsum = sums
            inner = pl.ds(pl.multiple_of(i * LANES, LANES), LANES)
            outer = pl.ds(pl.multiple_of(p * width + i * LANES, LANES), LANES)
            grad = own[y, x, :, outer].astype(jnp.float32)
            if along_x:
                for k in range(n_x - 1):
                    grad += r1a[p // 2, k, y, :, inner].astype(jnp.float32)
                for k in range(n_y - 1):
                    grad += r2a[p // 2, k, :, inner].astype(jnp.float32)
            else:
                for k in range(n_y - 1):
                    grad += r1b[p // 2, k, x, :, inner].astype(jnp.float32)
                for k in range(n_x - 1):
                    grad += r2b[p // 2, k, :, inner].astype(jnp.float32)
            weights = p_v[:, outer].astype(jnp.float32)
            old1, old2 = m1_v[:, outer], m2_v[:, outer]
            first = 0.9 * old1 + 0.1 * grad
            second = 0.99 * old2 + 0.01 * grad * grad
            update = first * (1.0 / bias_first) / (jnp.sqrt(second * (1.0 / bias_second)) + 1e-06) + row_decay * weights
            upd[:, outer] = update
            new1_ref[:, outer] = jnp.where(row_live, first, old1)
            new2_ref[:, outer] = jnp.where(row_live, second, old2)
            return usum + update * update, wsum + weights * weights

        sums = lax.fori_loop(0, width // LANES, update_piece, sums, unroll=2)
        if p < n_sec:
            relay(p + 1)

    for d in range(pieces, n_sec):
        relay(d + 1)

    n_layer = decay_ref.shape[0]
    lane = lax.broadcasted_iota(jnp.int32, (1, LANES), 1)
    lines = []
    for b in range(blocks):
        chosen = jnp.where(lives[b] > 0, layers[b], -LANES)
        for q, values in enumerate((sums[1], sums[0])):
            block = values[b * block_rows : (b + 1) * block_rows]
            lines.append(jnp.where(lane == chosen + q * n_layer, jnp.sum(block, axis=1, keepdims=True), 0.0))
    line = jnp.sum(sum(lines[1:], lines[0]), axis=0, keepdims=True)

    def all_sum(line, slots, send_sem, recv_sem, index, peers):
        slots[index] = line
        copies = []
        for j, peer in enumerate(peers):
            c = pltpu.make_async_remote_copy(
                src_ref=slots.at[index], dst_ref=slots.at[index],
                send_sem=send_sem.at[j], recv_sem=recv_sem.at[j],
                device_id=peer, device_id_type=MESH,
            )
            c.start()
            copies.append(c)
        for c in copies:
            c.wait_recv()
        total = slots[0]
        for j in range(1, len(peers) + 1):
            total += slots[j]
        return total, copies

    shard_peers = [(sec, lax.rem(me + j, n_shard)) for j in range(1, n_shard)]
    sec_peers = [(lax.rem(sec + j, n_sec), me) for j in range(1, n_sec)]
    if ONE_SHOT and n_shard * n_sec <= 32:
        every = [
            (lax.rem(sec + i, n_sec), lax.rem(me + j, n_shard))
            for i in range(n_sec) for j in range(n_shard) if i or j
        ]
        line, sends = all_sum(line, tiles, t_send, t_recv, sec * n_shard + me, every)
    else:
        line, sends = all_sum(line, tiles, t_send, t_recv, me, shard_peers)
        line, zsends = all_sum(line, ztiles, z_send, z_recv, sec, sec_peers)
        sends += zsends
    ratios = jnp.sqrt(line / (pltpu.roll(line, LANES - n_layer, 1) + 1.0))
    ratio_ref[...] = ratios
    step_ref[...] = jnp.concatenate(
        [
            jnp.broadcast_to(
                0.1 * jnp.sum(
                    jnp.where((lane == layers[b]) & (lives[b] > 0), ratios, 0.0), axis=1, keepdims=True
                ),
                (block_rows, LANES),
            )
            for b in range(blocks)
        ],
        axis=0,
    )

    for c in pair + [c for group in raws + ones + twos for c in group] + sends:
        c.wait_send()


def finish(parts, p_v, upd, new1_v, new2_v, step_v, ratio_v, newp_hbm, new1_hbm, new2_hbm, ratio_ref, newp_v, sem):
    cols = p_v.shape[1]
    width = cols // parts
    copies = []
    for k in range(parts):
        span = pl.ds(k * width, width)
        for i, (src, dst) in enumerate(((new1_v, new1_hbm), (new2_v, new2_hbm))):
            c = pltpu.make_async_copy(src.at[:, span], dst.at[:, span], sem.at[i, k])
            c.start()
            copies.append(c)
    ratio_ref[...] = ratio_v[0, : ratio_ref.shape[0]]
    row_step = step_v[...]

    for k in range(parts):
        def step_piece(i, carry, k=k):
            outer = pl.ds(pl.multiple_of(k * width + i * LANES, LANES), LANES)
            stepped = p_v[:, outer].astype(jnp.float32) - row_step * upd[:, outer]
            newp_v[:, outer] = stepped.astype(jnp.bfloat16)
            return carry

        lax.fori_loop(0, width // LANES, step_piece, 0, unroll=4)
        span = pl.ds(k * width, width)
        c = pltpu.make_async_copy(newp_v.at[:, span], newp_hbm.at[:, span], sem.at[2, k])
        c.start()
        copies.append(c)
    for c in copies:
        c.wait()


def shards(grad_parts, params, moment_first, moment_second, block_layer, block_valid, decay):
    n_sec, n_shard = lax.axis_size("section"), lax.axis_size("shard")
    chips = n_shard // 2
    n_y = max(d for d in range(1, math.isqrt(chips) + 1) if chips % d == 0)
    n_x = chips // n_y
    rows, cols = params.shape[1:]
    n_layer = decay.shape[0]
    pieces = PIECES
    half, width = pieces // 2, cols // pieces
    raw = width * 3 // 8 // LANES * LANES
    bf16, f32 = jnp.bfloat16, jnp.float32
    dma = pltpu.SemaphoreType.DMA
    n_lines = n_shard * n_sec if ONE_SHOT and n_shard * n_sec <= 32 else n_shard
    most = max(n_x, n_y) - 1
    grads = grad_parts.reshape(n_y, n_x, 2, rows, cols)
    any_spec = pl.BlockSpec(memory_space=pltpu.HBM)
    smem = pl.BlockSpec(memory_space=pltpu.SMEM)
    vmem = pl.BlockSpec(memory_space=pltpu.VMEM)
    held = pl.pallas_call(
        functools.partial(kernel, n_sec, n_y, n_x, pieces),
        out_shape=(
            pltpu.VMEM((rows, cols), bf16),
            pltpu.VMEM((rows, cols), f32),
            pltpu.VMEM((rows, cols), f32),
            pltpu.VMEM((rows, cols), f32),
            pltpu.VMEM((rows, LANES), f32),
            pltpu.VMEM((1, LANES), f32),
        ),
        in_specs=[any_spec] * 4 + [smem] * 3,
        out_specs=(vmem,) * 6,
        scratch_shapes=[
            pltpu.VMEM((n_y, n_x, rows, cols), bf16),
            pltpu.VMEM((n_y, n_x, rows, cols), bf16),
            pltpu.VMEM((n_y, n_x, rows, cols), bf16),
            pltpu.VMEM((rows, cols), f32),
            pltpu.VMEM((rows, cols), f32),
            pltpu.VMEM((half, n_x - 1, n_y, rows, width), bf16),
            pltpu.VMEM((half, n_y - 1, n_x, rows, width), bf16),
            pltpu.VMEM((half, n_y - 1, rows, width), bf16),
            pltpu.VMEM((half, n_x - 1, rows, width), bf16),
            pltpu.VMEM((half, n_y - 1, rows, width), bf16),
            pltpu.VMEM((half, n_x - 1, rows, width), bf16),
            pltpu.VMEM((n_lines, 1, LANES), f32),
            pltpu.VMEM((n_sec, 1, LANES), f32),
            dma((2, pieces)),
            dma((3,)),
            dma((2, pieces)),
            dma((pieces, most)),
            dma((pieces, most)),
            dma((pieces, most)),
            dma((pieces, most)),
            dma((n_lines - 1,)),
            dma((n_lines - 1,)),
            dma((n_sec - 1,)),
            dma((n_sec - 1,)),
            pltpu.SemaphoreType.REGULAR((2, n_sec - 1)),
            pltpu.VMEM((n_x - 1, n_y, rows, raw), bf16),
            pltpu.VMEM((n_y - 1, n_x, rows, raw), bf16),
            dma((2, 2, most)),
            dma((2, 2, most)),
        ],
        compiler_params=pltpu.CompilerParams(
            collective_id=0, has_side_effects=True, vmem_limit_bytes=56 * 1024 * 1024
        ),
    )(grads, params[0], moment_first[0], moment_second[0], block_layer, block_valid, decay)
    out = pl.pallas_call(
        functools.partial(finish, PARTS),
        out_shape=(
            jax.ShapeDtypeStruct((rows, cols), bf16),
            jax.ShapeDtypeStruct((rows, cols), f32),
            jax.ShapeDtypeStruct((rows, cols), f32),
            jax.ShapeDtypeStruct((n_layer,), f32),
        ),
        in_specs=[vmem] * 6,
        out_specs=(any_spec, any_spec, any_spec, vmem),
        scratch_shapes=[pltpu.VMEM((rows, cols), bf16), dma((3, PARTS))],
        compiler_params=pltpu.CompilerParams(vmem_limit_bytes=8 * 1024 * 1024),
    )(*held)
    return (out[0][None], out[1][None], out[2][None], out[3])


def solution(mesh):
    placed = (
        P("section", "shard", None, None),
        P("section", "shard", None),
        P("section", "shard", None),
        P("section", "shard", None),
        P("section", "shard"),
        P("section", "shard"),
        P(),
    )
    return jax.shard_map(
        shards,
        mesh=mesh,
        in_specs=placed,
        out_specs=(
            P("section", "shard", None),
            P("section", "shard", None),
            P("section", "shard", None),
            P(),
        ),
        check_vma=False,
    )
```

profile of v0, /device:TPU:0, one launch (start us, length us, event | category | flops | bytes accessed | tf_op | source)
XLA Modules:
  0.0 35.1 jit_solution(13872892829003689602)
XLA Ops:
  0.6 32.4 %shard_map.102 = (bf16[32,8192]{1,0:T(8,128)(2,1)S(1)}, f32[32,8192]{1,0:T(8,128)S(1)}, f32[32,8192]{1,0:T(8,128)S(1)}, f32[32,8192]{1,0:T(8,128)S(1)}, f32[32,128]{1,0:T(8,128)S(1)}, /*index=5*/f32[1,128]{1,0:T(1,128)S(1)}) custom-call(bf16[2,2,2,32,8192]{4,3,2,1,0:T(8,128)(2,1)} %bitcast.7, bf16[32,8192]{1,0:T(8,128)(2,1)} %bitcast.10, ...), custom_call_target="tpu_custom_call" | custom-call | tf_op jit(solution)/shard_map/pallas_call | solution.py:374
  33.1 2.0 %shard_map.103 = (bf16[32,8192]{1,0:T(8,128)(2,1)}, f32[32,8192]{1,0:T(8,128)}, f32[32,8192]{1,0:T(8,128)}, f32[8]{0:T(128)}) custom-call(bf16[32,8192]{1,0:T(8,128)(2,1)S(1)} %get-tuple-element.14.p_v, f32[32,8192]{1,0:T(8,128)S(1)} %get-tuple-element.15.upd, f32[32,8192]{1,0:T(8,128)S(1)} %get-tuple-element.16.new1_v, ...), custom_call_target="tpu_custom_call" | custom-call | tf_op jit(solution)/shard_map/pallas_call | solution.py:421
where the time goes:
time: 35.3 us; the launch traced here: 35.1 us
  Pallas kernels  34.5 us (98%)
  between operations  0.64 us (2%)
    pallas_call x1, Pallas kernels, shards(): pl.pallas_call(functools.partial(kernel, n_sec, n_y, n_x, pieces), out_sh...  32.4 us
    pallas_call x1, Pallas kernels, shards(): pl.pallas_call(functools.partial(finish, PARTS), out_shape=(jax.ShapeDtyp...  2.04 us

commit v1 on v0

v1 whole, which is shorter than its diff:
```python
import functools
import math

import jax
import jax.numpy as jnp
from jax import lax
from jax.experimental import pallas as pl
from jax.experimental.pallas import tpu as pltpu
from jax.sharding import PartitionSpec as P

MESH = pl.DeviceIdType.MESH
bias_first = 1.0 - 0.9**10
bias_second = 1.0 - 0.99**10
LANES = 128
CUTS = (2, 7, 17, 27, 32)
ONE_SHOT = True
PARTS = 2


def kernel(
    n_sec, n_y, n_x, cuts,
    g_hbm, p_hbm, m1_hbm, m2_hbm, layer_hbm, valid_hbm, decay_hbm,
    p_v, upd, new1_ref, new2_ref, step_ref, ratio_ref,
    mine, d2d, m1_v, m2_v, r1x, r1y, s1x, s1y, r2x, r2y, xa, ya, tiles, ztiles, layer_ref, valid_ref, decay_ref,
    pair_recv, one_recv, two_recv, raw_recv, t_recv, z_recv, told,
):
    count = len(cuts)
    most = max(n_x, n_y) - 1
    one_shot = ztiles is None
    dma = pltpu.SemaphoreType.DMA
    pl.run_scoped(
        functools.partial(
            body, n_sec, n_y, n_x, cuts, one_shot,
            g_hbm, p_hbm, m1_hbm, m2_hbm, layer_hbm, valid_hbm, decay_hbm,
            p_v, upd, new1_ref, new2_ref, step_ref, ratio_ref,
            mine, d2d, m1_v, m2_v, (r1x, r1y), (s1x, s1y), (r2x, r2y), (xa, ya), tiles, ztiles,
            layer_ref, valid_ref, decay_ref,
            pair_recv, one_recv, two_recv, raw_recv, t_recv, z_recv, told,
        ),
        load_sem=dma((count, 2)),
        state_sem=dma((6,)),
        pair_send=dma((count, 2)),
        one_send=dma((count, 2, most)),
        two_send=dma((count, 2, most)),
        raw_send=dma((2, most)),
        t_send=dma((1,)),
        z_send=dma((1,)),
    )


def body(
    n_sec, n_y, n_x, cuts, one_shot,
    g_hbm, p_hbm, m1_hbm, m2_hbm, layer_hbm, valid_hbm, decay_hbm,
    p_v, upd, new1_ref, new2_ref, step_ref, ratio_ref,
    mine, d2d, m1_v, m2_v, r1, s1, r2, other, tiles, ztiles, layer_ref, valid_ref, decay_ref,
    pair_recv, one_recv, two_recv, raw_recv, t_recv, z_recv, told,
    load_sem, state_sem, pair_send, one_send, two_send, raw_send, t_send, z_send,
):
    rows, cols = p_v.shape
    half = cols // 2
    count = len(cuts)
    n_shard = 2 * n_y * n_x
    sec, me = lax.axis_index("section"), lax.axis_index("shard")
    core = lax.rem(me, 2)
    x = lax.rem(me // 2, n_x)
    y = me // (2 * n_x)
    blocks = layer_ref.shape[1]
    block_rows = rows // blocks

    def at(yy, xx, cc):
        return (sec, (yy * n_x + xx) * 2 + cc)

    starts = (0,) + cuts[:-1]

    def span(k, d):
        return pl.ds(d * half + starts[k], cuts[k] - starts[k])

    def inner(k):
        return pl.ds(starts[k], cuts[k] - starts[k])

    loads = {}
    for k in range(count):
        for d in range(2):
            c = pltpu.make_async_copy(
                g_hbm.at[:, :, :, :, span(k, d)], mine.at[:, :, :, :, span(k, d)], load_sem.at[k, d]
            )
            c.start()
            loads[k, d] = c
        if k == 0:
            barrier = pltpu.get_barrier_semaphore()
            near = [at(y, x, 1 - core)]
            for cc in (core, 1 - core):
                near += [at(y, lax.rem(x + j, n_x), cc) for j in range(1, n_x)]
                near += [at(lax.rem(y + j, n_y), x, cc) for j in range(1, n_y)]
            for peer in near:
                pl.semaphore_signal(barrier, inc=1, device_id=peer, device_id_type=MESH)
            last_sec = n_sec - 1
            up = (jnp.minimum(sec + 1, last_sec), me)
            down = (jnp.maximum(sec - 1, 0), me)

            @pl.when(sec < last_sec)
            def _():
                pl.semaphore_signal(barrier, inc=1, device_id=up, device_id_type=MESH)

            @pl.when(sec > 0)
            def _():
                pl.semaphore_signal(barrier, inc=1, device_id=down, device_id_type=MESH)

    states = [
        pltpu.make_async_copy(src, dst, state_sem.at[i])
        for i, (src, dst) in enumerate(
            (
                (layer_hbm, layer_ref), (valid_hbm, valid_ref), (decay_hbm, decay_ref),
                (p_hbm, p_v), (m1_hbm, m1_v), (m2_hbm, m2_v),
            )
        )
    ]
    for s in states:
        s.start()

    ends = jnp.where(sec < last_sec, 1, 0) + jnp.where(sec > 0, 1, 0)
    with jax.named_scope("bar"):
        pl.semaphore_wait(barrier, len(near) + ends)

    def relay(d):
        if 1 < d <= n_sec:

            @pl.when(sec >= d - 1)
            def _():
                pl.semaphore_wait(told.at[0, d - 2], 1)

            @pl.when(sec <= n_sec - d)
            def _():
                pl.semaphore_wait(told.at[1, d - 2], 1)

        if d < n_sec:

            @pl.when((sec >= d - 1) & (sec < last_sec))
            def _():
                pl.semaphore_signal(told.at[0, d - 1], inc=1, device_id=up, device_id_type=MESH)

            @pl.when((sec <= n_sec - d) & (sec > 0))
            def _():
                pl.semaphore_signal(told.at[1, d - 1], inc=1, device_id=down, device_id_type=MESH)

    def place(d, t):
        return (slice(None), t) if d == 0 else (t, slice(None))

    def peer_at(d, t, cc):
        return at(y, t, cc) if d == 0 else at(t, x, cc)

    here = (x, y)
    first_n, second_n = (n_x, n_y), (n_y, n_x)

    ones = {(k, d): [] for k in range(count) for d in range(2)}
    raws = {0: [], 1: []}
    for d in range(2):
        with jax.named_scope(f"ldw0{d}"):
            loads[0, d].wait()
        for j in range(1, first_n[d]):
            t = lax.rem(here[d] + j, first_n[d])
            c = pltpu.make_async_remote_copy(
                src_ref=mine.at[(*place(d, t), core, slice(None), span(0, d))],
                dst_ref=r1[d].at[j - 1, :, :, inner(0)],
                send_sem=one_send.at[0, d, j - 1], recv_sem=one_recv.at[0, d, j - 1],
                device_id=peer_at(d, t, core), device_id_type=MESH,
            )
            c.start()
            ones[0, d].append(c)
            c = pltpu.make_async_remote_copy(
                src_ref=mine.at[(*place(d, t), 1 - core, slice(None), span(0, d))],
                dst_ref=other[d].at[j - 1],
                send_sem=raw_send.at[d, j - 1], recv_sem=raw_recv.at[d, j - 1],
                device_id=peer_at(d, t, 1 - core), device_id_type=MESH,
            )
            c.start()
            raws[d].append(c)

    pair = {}

    def send_pair(k, d):
        if k:
            with jax.named_scope(f"ldw{k}{d}"):
                loads[k, d].wait()
        t = slice(None) if k else here[d]
        spot = place(d, t)
        c = pltpu.make_async_remote_copy(
            src_ref=mine.at[(*spot, 1 - core, slice(None), span(k, d))],
            dst_ref=d2d.at[(*spot, slice(None), span(k, d))],
            send_sem=pair_send.at[k, d], recv_sem=pair_recv.at[k, d],
            device_id=at(y, x, 1 - core), device_id_type=MESH,
        )
        c.start()
        pair[k, d] = c

    def add_pair(yy, xx, cut):
        total = mine[yy, xx, core, :, cut].astype(jnp.float32) + d2d[yy, xx, :, cut].astype(jnp.float32)
        mine[yy, xx, core, :, cut] = total.astype(jnp.bfloat16)

    def send_one(k, d):
        with jax.named_scope(f"pairw{k}{d}"):
            pair[k, d].wait_recv()
        cut = span(k, d)

        def add_all(i, carry):
            add_pair(i // n_x, lax.rem(i, n_x), cut)
            return carry

        lax.fori_loop(0, n_y * n_x, add_all, 0)
        for j in range(1, first_n[d]):
            t = lax.rem(here[d] + j, first_n[d])
            c = pltpu.make_async_remote_copy(
                src_ref=mine.at[(*place(d, t), core, slice(None), cut)],
                dst_ref=r1[d].at[j - 1, :, :, inner(k)],
                send_sem=one_send.at[k, d, j - 1], recv_sem=one_recv.at[k, d, j - 1],
                device_id=peer_at(d, t, core), device_id_type=MESH,
            )
            c.start()
            ones[k, d].append(c)

    ahead = 2
    for k in range(1, 1 + ahead):
        for d in range(2):
            send_pair(k, d)
    for d in range(2):
        send_pair(0, d)
    for k in range(1, count):
        for d in range(2):
            send_one(k, d)
        if k + ahead < count:
            for d in range(2):
                send_pair(k + ahead, d)
    for d in range(2):
        pair[0, d].wait_recv()
        for i in range(second_n[d]):
            add_pair(i if d == 0 else y, x if d == 0 else i, span(0, d))

    def partial(k, d, t, cut, near_cut, raw_cut):
        yy, xx = (t, x) if d == 0 else (y, t)
        total = mine[yy, xx, core, :, cut].astype(jnp.float32)
        for i in range(first_n[d] - 1):
            total += r1[d][i, t, :, near_cut].astype(jnp.float32)
            if k == 0:
                total += other[d][i, t, :, raw_cut].astype(jnp.float32)
        return total

    twos = {}
    for k in range(count):
        for d in range(2):
            with jax.named_scope(f"onew{k}{d}"):
                for c in ones[k, d]:
                    c.wait_recv()
                if k == 0:
                    for c in raws[d]:
                        c.wait_recv()
            group = []
            for j in range(1, second_n[d]):
                at_hand = y if d == 0 else x
                t = lax.rem(at_hand + j, second_n[d])
                total = partial(k, d, t, span(k, d), inner(k), slice(None))
                s1[d][j - 1, :, inner(k)] = total.astype(jnp.bfloat16)
                c = pltpu.make_async_remote_copy(
                    src_ref=s1[d].at[j - 1, :, inner(k)], dst_ref=r2[d].at[j - 1, :, inner(k)],
                    send_sem=two_send.at[k, d, j - 1], recv_sem=two_recv.at[k, d, j - 1],
                    device_id=peer_at(1 - d, t, core), device_id_type=MESH,
                )
                c.start()
                group.append(c)
            twos[k, d] = group
        if k < n_sec:
            relay(k + 1)
    for k in range(count, n_sec):
        relay(k + 1)

    def by_block(scalars):
        return jnp.concatenate([jnp.full((block_rows, LANES), s) for s in scalars], axis=0)

    for s in states:
        s.wait()
    layers = [layer_ref[0, b] for b in range(blocks)]
    lives = [valid_ref[0, b] for b in range(blocks)]
    row_decay = by_block([decay_ref[layer] for layer in layers])
    row_live = by_block([jnp.where(v > 0, 1.0, 0.0).astype(jnp.float32) for v in lives]) > 0.5
    for d in range(2):
        for c in raws[d]:
            c.wait_send()
    for k in range(count):
        for d in range(2):
            pair[k, d].wait_send()

    zero = jnp.zeros((rows, LANES), jnp.float32)
    sums = (zero, zero)
    for k in range(count):
        for d in range(2):
            with jax.named_scope(f"twow{k}{d}"):
                for c in twos[k, d]:
                    c.wait_recv()

            def update_piece(i, sums, k=k, d=d):
                usum, wsum = sums
                raw_cut = pl.ds(pl.multiple_of(i * LANES, LANES), LANES)
                near_cut = pl.ds(pl.multiple_of(starts[k] + i * LANES, LANES), LANES)
                cut = pl.ds(pl.multiple_of(d * half + starts[k] + i * LANES, LANES), LANES)
                grad = partial(k, d, y if d == 0 else x, cut, near_cut, raw_cut)
                for j in range(second_n[d] - 1):
                    grad += r2[d][j, :, near_cut].astype(jnp.float32)
                weights = p_v[:, cut].astype(jnp.float32)
                old1, old2 = m1_v[:, cut], m2_v[:, cut]
                first = 0.9 * old1 + 0.1 * grad
                second = 0.99 * old2 + 0.01 * grad * grad
                update = first * (1.0 / bias_first) / (jnp.sqrt(second * (1.0 / bias_second)) + 1e-06)
                update += row_decay * weights
                upd[:, cut] = update
                new1_ref[:, cut] = jnp.where(row_live, first, old1)
                new2_ref[:, cut] = jnp.where(row_live, second, old2)
                return usum + update * update, wsum + weights * weights

            n = (cuts[k] - starts[k]) // LANES
            with jax.named_scope(f"upd{k}{d}"):
                sums = lax.fori_loop(0, n, update_piece, sums, unroll=2 if n % 2 == 0 else 1)

    n_layer = decay_ref.shape[0]
    lane = lax.broadcasted_iota(jnp.int32, (1, LANES), 1)
    lines = []
    for b in range(blocks):
        chosen = jnp.where(lives[b] > 0, layers[b], -LANES)
        for q, values in enumerate((sums[1], sums[0])):
            block = values[b * block_rows : (b + 1) * block_rows]
            lines.append(jnp.where(lane == chosen + q * n_layer, jnp.sum(block, axis=1, keepdims=True), 0.0))
    line = jnp.sum(sum(lines[1:], lines[0]), axis=0, keepdims=True)

    def all_sum(line, slots, send_sem, recv_sem, index, peers):
        slots[index] = line
        for peer in peers:
            pltpu.make_async_remote_copy(
                src_ref=slots.at[index], dst_ref=slots.at[index],
                send_sem=send_sem.at[0], recv_sem=recv_sem.at[0],
                device_id=peer, device_id_type=MESH,
            ).start()
        whole = slots.at[pl.ds(0, len(peers))]
        both = pltpu.make_async_remote_copy(
            src_ref=whole, dst_ref=whole, send_sem=send_sem.at[0], recv_sem=recv_sem.at[0],
            device_id=peers[0], device_id_type=MESH,
        )
        with jax.named_scope("allw"):
            both.wait_recv()
        terms = [slots[j] for j in range(len(peers) + 1)]
        while len(terms) > 1:
            terms = [sum(terms[i + 1 : i + 2], terms[i]) for i in range(0, len(terms), 2)]
        return terms[0], both

    if one_shot:
        every = [
            (lax.rem(sec + i, n_sec), lax.rem(me + j, n_shard))
            for i in (*range(1, n_sec), 0) for j in range(n_shard) if i or j
        ]
        line, sent = all_sum(line, tiles, t_send, t_recv, sec * n_shard + me, every)
        sends = [sent]
    else:
        shard_peers = [(sec, lax.rem(me + j, n_shard)) for j in range(1, n_shard)]
        sec_peers = [(lax.rem(sec + j, n_sec), me) for j in range(1, n_sec)]
        line, sent = all_sum(line, tiles, t_send, t_recv, me, shard_peers)
        line, zsent = all_sum(line, ztiles, z_send, z_recv, sec, sec_peers)
        sends = [sent, zsent]
    ratios = jnp.sqrt(line / (pltpu.roll(line, LANES - n_layer, 1) + 1.0))
    ratio_ref[...] = ratios[0, :n_layer]
    step_ref[...] = jnp.concatenate(
        [
            jnp.broadcast_to(
                0.1 * jnp.sum(
                    jnp.where((lane == layers[b]) & (lives[b] > 0), ratios, 0.0), axis=1, keepdims=True
                ),
                (block_rows, LANES),
            )
            for b in range(blocks)
        ],
        axis=0,
    )
    with jax.named_scope("endw"):
        for group in (*ones.values(), *twos.values(), sends):
            for c in group:
                c.wait_send()


def finish(parts, p_v, upd, new1_v, new2_v, step_v, ratio_v, newp_hbm, new1_hbm, new2_hbm, ratio_hbm, newp_v, sem):
    cols = p_v.shape[1]
    width = cols // parts
    copies = []
    for i, (src, dst) in enumerate(((ratio_v, ratio_hbm), (new1_v, new1_hbm), (new2_v, new2_hbm))):
        c = pltpu.make_async_copy(src, dst, sem.at[i])
        c.start()
        copies.append(c)
    row_step = step_v[...]

    for k in range(parts):
        def step_piece(i, carry, k=k):
            outer = pl.ds(pl.multiple_of(k * width + i * LANES, LANES), LANES)
            stepped = p_v[:, outer].astype(jnp.float32) - row_step * upd[:, outer]
            newp_v[:, outer] = stepped.astype(jnp.bfloat16)
            return carry

        lax.fori_loop(0, width // LANES, step_piece, 0, unroll=4)
        span = pl.ds(k * width, width)
        c = pltpu.make_async_copy(newp_v.at[:, span], newp_hbm.at[:, span], sem.at[3 + k])
        c.start()
        copies.append(c)
    for c in copies:
        c.wait()


def shards(grad_parts, params, moment_first, moment_second, block_layer, block_valid, decay):
    n_sec, n_shard = lax.axis_size("section"), lax.axis_size("shard")
    chips = n_shard // 2
    n_y = max(d for d in range(1, math.isqrt(chips) + 1) if chips % d == 0)
    n_x = chips // n_y
    rows, cols = params.shape[1:]
    n_layer = decay.shape[0]
    half = cols // 2
    cuts = tuple(half // LANES * c // CUTS[-1] * LANES for c in CUTS)
    count = len(cuts)
    bf16, f32 = jnp.bfloat16, jnp.float32
    dma = pltpu.SemaphoreType.DMA
    one_shot = ONE_SHOT and n_shard * n_sec <= 32
    n_lines = n_shard * n_sec if one_shot else n_shard
    most = max(n_x, n_y) - 1
    grads = grad_parts.reshape(n_y, n_x, 2, rows, cols)
    any_spec = pl.BlockSpec(memory_space=pltpu.HBM)
    vmem = pl.BlockSpec(memory_space=pltpu.VMEM)
    held = pl.pallas_call(
        functools.partial(kernel, n_sec, n_y, n_x, cuts),
        out_shape=(
            pltpu.VMEM((rows, cols), bf16),
            pltpu.VMEM((rows, cols), f32),
            pltpu.VMEM((rows, cols), f32),
            pltpu.VMEM((rows, cols), f32),
            pltpu.VMEM((rows, LANES), f32),
            pltpu.VMEM((n_layer,), f32),
        ),
        in_specs=[any_spec] * 7,
        out_specs=(vmem,) * 6,
        scratch_shapes=[
            pltpu.VMEM((n_y, n_x, 2, rows, cols), bf16),
            pltpu.VMEM((n_y, n_x, rows, cols), bf16),
            pltpu.VMEM((rows, cols), f32),
            pltpu.VMEM((rows, cols), f32),
            pltpu.VMEM((n_x - 1, n_y, rows, half), bf16),
            pltpu.VMEM((n_y - 1, n_x, rows, half), bf16),
            pltpu.VMEM((n_y - 1, rows, half), bf16),
            pltpu.VMEM((n_x - 1, rows, half), bf16),
            pltpu.VMEM((n_y - 1, rows, half), bf16),
            pltpu.VMEM((n_x - 1, rows, half), bf16),
            pltpu.VMEM((n_x - 1, n_y, rows, cuts[0]), bf16),
            pltpu.VMEM((n_y - 1, n_x, rows, cuts[0]), bf16),
            pltpu.VMEM((n_lines, 1, LANES), f32),
            None if one_shot else pltpu.VMEM((n_sec, 1, LANES), f32),
            pltpu.SMEM(block_layer.shape, jnp.int32),
            pltpu.SMEM(block_valid.shape, jnp.int32),
            pltpu.SMEM(decay.shape, f32),
            dma((count, 2)),
            dma((count, 2, most)),
            dma((count, 2, most)),
            dma((2, most)),
            dma((1,)),
            dma((1,)),
            pltpu.SemaphoreType.REGULAR((2, n_sec - 1)),
        ],
        compiler_params=pltpu.CompilerParams(
            collective_id=0, has_side_effects=True, vmem_limit_bytes=56 * 1024 * 1024
        ),
    )(grads, params[0], moment_first[0], moment_second[0], block_layer, block_valid, decay)
    out = pl.pallas_call(
        functools.partial(finish, PARTS),
        out_shape=(
            jax.ShapeDtypeStruct((rows, cols), bf16),
            jax.ShapeDtypeStruct((rows, cols), f32),
            jax.ShapeDtypeStruct((rows, cols), f32),
            jax.ShapeDtypeStruct((n_layer,), f32),
        ),
        in_specs=[vmem] * 6,
        out_specs=(any_spec,) * 4,
        scratch_shapes=[pltpu.VMEM((rows, cols), bf16), dma((3 + PARTS,))],
        compiler_params=pltpu.CompilerParams(vmem_limit_bytes=8 * 1024 * 1024),
    )(*held)
    return (out[0][None], out[1][None], out[2][None], out[3])


def solution(mesh):
    placed = (
        P("section", "shard", None, None),
        P("section", "shard", None),
        P("section", "shard", None),
        P("section", "shard", None),
        P("section", "shard"),
        P("section", "shard"),
        P(),
    )
    return jax.shard_map(
        shards,
        mesh=mesh,
        in_specs=placed,
        out_specs=(
            P("section", "shard", None),
            P("section", "shard", None),
            P("section", "shard", None),
            P(),
        ),
        check_vma=False,
    )
```

time: 35.3 us -> 32.7 us (0.926)
  Pallas kernels: 34.5 us -> 31.9 us
    pallas_call x1, Pallas kernels: 32.4 us -> 30.3 us  [shards(): pl.pallas_call(functools.partial(kernel, n_sec, n_y, n_x, cuts), out_shap...]
    pallas_call x1, Pallas kernels: 2.04 us -> 1.53 us  [shards(): pl.pallas_call(functools.partial(finish, PARTS), out_shape=(jax.ShapeDtyp...]
where the time goes in v1:
time: 32.7 us; the launch traced here: 32.5 us
  Pallas kernels  31.9 us (98%)
  between operations  0.64 us (2%)
    pallas_call x1, Pallas kernels, shards(): pl.pallas_call(functools.partial(kernel, n_sec, n_y, n_x, cuts), out_shap...  30.3 us
    pallas_call x1, Pallas kernels, shards(): pl.pallas_call(functools.partial(finish, PARTS), out_shape=(jax.ShapeDtyp...  1.53 us

profile of v1, /device:TPU:0, one launch (start us, length us, event | category | flops | bytes accessed | tf_op | source)
XLA Modules:
  0.0 32.5 jit_solution(11873486474649081419)
XLA Ops:
  0.6 30.3 %shard_map.102 = (bf16[32,8192]{1,0:T(8,128)(2,1)S(1)}, f32[32,8192]{1,0:T(8,128)S(1)}, f32[32,8192]{1,0:T(8,128)S(1)}, f32[32,8192]{1,0:T(8,128)S(1)}, f32[32,128]{1,0:T(8,128)S(1)}, /*index=5*/f32[8]{0:T(128)S(1)}) custom-call(bf16[2,2,2,32,8192]{4,3,2,1,0:T(8,128)(2,1)} %bitcast.7, bf16[32,8192]{1,0:T(8,128)(2,1)} %bitcast.10, f32[32,8192]{1,0:T(8,128)} %bitcast.8, ...), custom_call_target="tpu_custom_call" | custom-call | tf_op jit(solution)/shard_map/pallas_call | solution.py:429
  31.0 1.5 %shard_map.103 = (bf16[32,8192]{1,0:T(8,128)(2,1)}, f32[32,8192]{1,0:T(8,128)}, f32[32,8192]{1,0:T(8,128)}, f32[8]{0:T(128)}) custom-call(bf16[32,8192]{1,0:T(8,128)(2,1)S(1)} %get-tuple-element.14.p_v, f32[32,8192]{1,0:T(8,128)S(1)} %get-tuple-element.15.upd, f32[32,8192]{1,0:T(8,128)S(1)} %get-tuple-element.16.new1_v, ...), custom_call_target="tpu_custom_call" | custom-call | tf_op jit(solution)/shard_map/pallas_call | solution.py:471

commit v2 on v1

--- a/solution.py
+++ b/solution.py
@@ -11,18 +11,19 @@
 MESH = pl.DeviceIdType.MESH
 bias_first = 1.0 - 0.9**10
 bias_second = 1.0 - 0.99**10
+root_second = math.sqrt(bias_second)
 LANES = 128
-CUTS = (2, 7, 17, 27, 32)
+CUTS = (2, 4, 7, 15, 23, 29, 31, 32)
+SHIFT = 2
 ONE_SHOT = True
-PARTS = 2
+PARTS = 4
 
 
 def kernel(
     n_sec, n_y, n_x, cuts,
     g_hbm, p_hbm, m1_hbm, m2_hbm, layer_hbm, valid_hbm, decay_hbm,
     p_v, upd, new1_ref, new2_ref, step_ref, ratio_ref,
-    mine, d2d, m1_v, m2_v, r1x, r1y, s1x, s1y, r2x, r2y, xa, ya, tiles, ztiles, layer_ref, valid_ref, decay_ref,
-    pair_recv, one_recv, two_recv, raw_recv, t_recv, z_recv, told,
+    mine, d2d, m1_v, m2_v, r1x, r1y, s1x, s1y, r2x, r2y, xa, ya, xs, ys, tiles, ztiles, layer_ref, valid_ref, decay_ref,
 ):
     count = len(cuts)
     most = max(n_x, n_y) - 1
@@ -33,18 +34,26 @@
             body, n_sec, n_y, n_x, cuts, one_shot,
             g_hbm, p_hbm, m1_hbm, m2_hbm, layer_hbm, valid_hbm, decay_hbm,
             p_v, upd, new1_ref, new2_ref, step_ref, ratio_ref,
-            mine, d2d, m1_v, m2_v, (r1x, r1y), (s1x, s1y), (r2x, r2y), (xa, ya), tiles, ztiles,
+            mine, d2d, m1_v, m2_v, (r1x, r1y), (s1x, s1y), (r2x, r2y), (xa, ya), (xs, ys), tiles, ztiles,
             layer_ref, valid_ref, decay_ref,
-            pair_recv, one_recv, two_recv, raw_recv, t_recv, z_recv, told,
         ),
         load_sem=dma((count, 2)),
         state_sem=dma((6,)),
         pair_send=dma((count, 2)),
         one_send=dma((count, 2, most)),
         two_send=dma((count, 2, most)),
-        raw_send=dma((2, most)),
+        raw_send=dma((2, 2, most)),
+        lent_send=dma((2, 2, most)),
+        lent_recv=dma((2, most)),
         t_send=dma((1,)),
         z_send=dma((1,)),
+        pair_recv=dma((count, 2)),
+        one_recv=dma((count, 2, most)),
+        two_recv=dma((count, 2, most)),
+        raw_recv=dma((2, most)),
+        t_recv=dma((1,)),
+        z_recv=dma((1,)),
+        told=pltpu.SemaphoreType.REGULAR((2, n_sec - 1)),
     )
 
 
@@ -52,9 +61,9 @@
     n_sec, n_y, n_x, cuts, one_shot,
     g_hbm, p_hbm, m1_hbm, m2_hbm, layer_hbm, valid_hbm, decay_hbm,
     p_v, upd, new1_ref, new2_ref, step_ref, ratio_ref,
-    mine, d2d, m1_v, m2_v, r1, s1, r2, other, tiles, ztiles, layer_ref, valid_ref, decay_ref,
+    mine, d2d, m1_v, m2_v, r1, s1, r2, other, lent, tiles, ztiles, layer_ref, valid_ref, decay_ref,
+    load_sem, state_sem, pair_send, one_send, two_send, raw_send, lent_send, lent_recv, t_send, z_send,
     pair_recv, one_recv, two_recv, raw_recv, t_recv, z_recv, told,
-    load_sem, state_sem, pair_send, one_send, two_send, raw_send, t_send, z_send,
 ):
     rows, cols = p_v.shape
     half = cols // 2
@@ -152,88 +161,166 @@
     here = (x, y)
     first_n, second_n = (n_x, n_y), (n_y, n_x)
 
-    ones = {(k, d): [] for k in range(count) for d in range(2)}
-    raws = {0: [], 1: []}
+    def others(d):
+        return [(j, lax.rem(here[d] + j, first_n[d])) for j in range(1, first_n[d])]
+
+    def remote(src, dst, send_sem, recv_sem, peer):
+        return pltpu.make_async_remote_copy(
+            src_ref=src, dst_ref=dst, send_sem=send_sem, recv_sem=recv_sem, device_id=peer, device_id_type=MESH
+        )
+
+    def rows_of(d, t, cc, k):
+        return mine.at[(*place(d, t), cc, slice(None), span(k, d))]
+
+    ones, raws, forwards, lends, crosses, pair, kept = {}, {}, {}, {}, {}, {}, {}
+    for d in range(2):
+        for k in range(count):
+            ones[k, d] = [
+                remote(
+                    rows_of(d, t, core, k), r1[d].at[j - 1, :, :, inner(k)],
+                    one_send.at[k, d, j - 1], one_recv.at[k, d, j - 1], peer_at(d, t, core),
+                )
+                for j, t in others(d)
+            ]
+            for group, t in ((pair, slice(None)), (kept, here[d])):
+                if group is kept and k not in (0, SHIFT):
+                    continue
+                spot = place(d, t)
+                group[k, d] = remote(
+                    rows_of(d, t, 1 - core, k), d2d.at[(*spot, slice(None), span(k, d))],
+                    pair_send.at[k, d], pair_recv.at[k, d], at(y, x, 1 - core),
+                )
+        raws[d] = [
+            remote(
+                rows_of(d, t, 1 - core, 0), other[d].at[j - 1],
+                raw_send.at[0, d, j - 1], raw_recv.at[d, j - 1], peer_at(d, t, 1 - core),
+            )
+            for j, t in others(d)
+        ]
+        forwards[d] = [
+            remote(
+                d2d.at[(*place(d, t), slice(None), span(0, d))], other[d].at[j - 1],
+                raw_send.at[1, d, j - 1], raw_recv.at[d, j - 1], peer_at(d, t, core),
+            )
+            for j, t in others(d)
+        ]
+        lends[d] = [
+            remote(
+                rows_of(d, t, core, SHIFT), lent[d].at[j - 1],
+                lent_send.at[0, d, j - 1], lent_recv.at[d, j - 1], at(y, x, 1 - core),
+            )
+            for j, t in others(d)
+        ]
+        crosses[d] = [
+            remote(
+                rows_of(d, t, 1 - core, SHIFT), r1[d].at[j - 1, :, :, inner(SHIFT)],
+                lent_send.at[1, d, j - 1], one_recv.at[SHIFT, d, j - 1], peer_at(d, t, 1 - core),
+            )
+            for j, t in others(d)
+        ]
+    is_far, is_near = core == 0, core == 1
+
     for d in range(2):
         with jax.named_scope(f"ldw0{d}"):
             loads[0, d].wait()
-        for j in range(1, first_n[d]):
-            t = lax.rem(here[d] + j, first_n[d])
-            c = pltpu.make_async_remote_copy(
-                src_ref=mine.at[(*place(d, t), core, slice(None), span(0, d))],
-                dst_ref=r1[d].at[j - 1, :, :, inner(0)],
-                send_sem=one_send.at[0, d, j - 1], recv_sem=one_recv.at[0, d, j - 1],
-                device_id=peer_at(d, t, core), device_id_type=MESH,
-            )
+        for c in ones[0, d]:
             c.start()
-            ones[0, d].append(c)
-            c = pltpu.make_async_remote_copy(
-                src_ref=mine.at[(*place(d, t), 1 - core, slice(None), span(0, d))],
-                dst_ref=other[d].at[j - 1],
-                send_sem=raw_send.at[d, j - 1], recv_sem=raw_recv.at[d, j - 1],
-                device_id=peer_at(d, t, 1 - core), device_id_type=MESH,
-            )
-            c.start()
-            raws[d].append(c)
-
-    pair = {}
+
+        @pl.when(is_near)
+        def _(d=d):
+            for c in raws[d]:
+                c.start()
 
     def send_pair(k, d):
         if k:
             with jax.named_scope(f"ldw{k}{d}"):
                 loads[k, d].wait()
-        t = slice(None) if k else here[d]
-        spot = place(d, t)
-        c = pltpu.make_async_remote_copy(
-            src_ref=mine.at[(*spot, 1 - core, slice(None), span(k, d))],
-            dst_ref=d2d.at[(*spot, slice(None), span(k, d))],
-            send_sem=pair_send.at[k, d], recv_sem=pair_recv.at[k, d],
-            device_id=at(y, x, 1 - core), device_id_type=MESH,
-        )
-        c.start()
-        pair[k, d] = c
+        if k in (0, SHIFT):
+
+            @pl.when(is_far)
+            def _():
+                pair[k, d].start()
+                if k:
+                    for c in lends[d]:
+                        c.start()
+
+            @pl.when(is_near)
+            def _():
+                kept[k, d].start()
+        else:
+            pair[k, d].start()
 
     def add_pair(yy, xx, cut):
         total = mine[yy, xx, core, :, cut].astype(jnp.float32) + d2d[yy, xx, :, cut].astype(jnp.float32)
         mine[yy, xx, core, :, cut] = total.astype(jnp.bfloat16)
 
-    def send_one(k, d):
-        with jax.named_scope(f"pairw{k}{d}"):
-            pair[k, d].wait_recv()
-        cut = span(k, d)
-
-        def add_all(i, carry):
+    def add_all(cut):
+        def add_one(i, carry):
             add_pair(i // n_x, lax.rem(i, n_x), cut)
             return carry
 
-        lax.fori_loop(0, n_y * n_x, add_all, 0)
-        for j in range(1, first_n[d]):
-            t = lax.rem(here[d] + j, first_n[d])
-            c = pltpu.make_async_remote_copy(
-                src_ref=mine.at[(*place(d, t), core, slice(None), cut)],
-                dst_ref=r1[d].at[j - 1, :, :, inner(k)],
-                send_sem=one_send.at[k, d, j - 1], recv_sem=one_recv.at[k, d, j - 1],
-                device_id=peer_at(d, t, core), device_id_type=MESH,
-            )
-            c.start()
-            ones[k, d].append(c)
-
-    ahead = 2
-    for k in range(1, 1 + ahead):
+        lax.fori_loop(0, n_y * n_x, add_one, 0)
+
+    def add_kept(d, cut):
+        for i in range(second_n[d]):
+            add_pair(i if d == 0 else y, x if d == 0 else i, cut)
+
+    def send_one(k, d):
+        cut = span(k, d)
+        if k == 0:
+
+            @pl.when(is_near)
+            def _():
+                pair[k, d].wait_recv()
+                for c in forwards[d]:
+                    c.start()
+
+            @pl.when(is_far)
+            def _():
+                kept[k, d].wait_recv()
+
+            add_kept(d, cut)
+        elif k == SHIFT:
+
+            @pl.when(is_near)
+            def _():
+                pair[k, d].wait_recv()
+                for c in lends[d]:
+                    c.wait_recv()
+                add_all(cut)
+                for c in ones[k, d]:
+                    c.start()
+                for j, t in others(d):
+                    for i in range(second_n[d]):
+                        yy, xx = (i, t) if d == 0 else (t, i)
+                        total = mine[yy, xx, 1 - core, :, cut].astype(jnp.float32)
+                        total += lent[d][j - 1, i].astype(jnp.float32)
+                        mine[yy, xx, 1 - core, :, cut] = total.astype(jnp.bfloat16)
+                for c in crosses[d]:
+                    c.start()
+
+            @pl.when(is_far)
+            def _():
+                kept[k, d].wait_recv()
+                add_kept(d, cut)
+        else:
+            with jax.named_scope(f"pairw{k}{d}"):
+                pair[k, d].wait_recv()
+            add_all(cut)
+            for c in ones[k, d]:
+                c.start()
+
+    ahead = 4
+    order = [1, 0, *range(2, count)]
+    for k in order[: 1 + ahead]:
         for d in range(2):
             send_pair(k, d)
-    for d in range(2):
-        send_pair(0, d)
-    for k in range(1, count):
+    for i, k in enumerate(order):
         for d in range(2):
             send_one(k, d)
-        if k + ahead < count:
+        if i + 1 + ahead < count:
             for d in range(2):
-                send_pair(k + ahead, d)
-    for d in range(2):
-        pair[0, d].wait_recv()
-        for i in range(second_n[d]):
-            add_pair(i if d == 0 else y, x if d == 0 else i, span(0, d))
+                send_pair(order[i + 1 + ahead], d)
 
     def partial(k, d, t, cut, near_cut, raw_cut):
         yy, xx = (t, x) if d == 0 else (y, t)
@@ -251,7 +338,7 @@
                 for c in ones[k, d]:
                     c.wait_recv()
                 if k == 0:
-                    for c in raws[d]:
+                    for c in forwards[d]:
                         c.wait_recv()
             group = []
             for j in range(1, second_n[d]):
@@ -282,11 +369,19 @@
     row_decay = by_block([decay_ref[layer] for layer in layers])
     row_live = by_block([jnp.where(v > 0, 1.0, 0.0).astype(jnp.float32) for v in lives]) > 0.5
     for d in range(2):
-        for c in raws[d]:
-            c.wait_send()
-    for k in range(count):
-        for d in range(2):
-            pair[k, d].wait_send()
+        for k in range(count):
+            if k not in (0, SHIFT):
+                pair[k, d].wait_send()
+
+        @pl.when(is_near)
+        def _(d=d):
+            for c in (kept[0, d], kept[SHIFT, d], *raws[d], *forwards[d], *ones[SHIFT, d], *crosses[d]):
+                c.wait_send()
+
+        @pl.when(is_far)
+        def _(d=d):
+            for c in (pair[0, d], pair[SHIFT, d], *lends[d]):
+                c.wait_send()
 
     zero = jnp.zeros((rows, LANES), jnp.float32)
     sums = (zero, zero)
@@ -306,10 +401,11 @@
                     grad += r2[d][j, :, near_cut].astype(jnp.float32)
                 weights = p_v[:, cut].astype(jnp.float32)
                 old1, old2 = m1_v[:, cut], m2_v[:, cut]
-                first = 0.9 * old1 + 0.1 * grad
-                second = 0.99 * old2 + 0.01 * grad * grad
-                update = first * (1.0 / bias_first) / (jnp.sqrt(second * (1.0 / bias_second)) + 1e-06)
-                update += row_decay * weights
+                tenth = 0.1 * grad
+                first = 0.9 * old1 + tenth
+                second = 0.99 * old2 + tenth * tenth
+                root = second * lax.rsqrt(second)
+                update = first * (root_second / bias_first) / (root + 1e-06 * root_second) + row_decay * weights
                 upd[:, cut] = update
                 new1_ref[:, cut] = jnp.where(row_live, first, old1)
                 new2_ref[:, cut] = jnp.where(row_live, second, old2)
@@ -317,20 +413,24 @@
 
             n = (cuts[k] - starts[k]) // LANES
             with jax.named_scope(f"upd{k}{d}"):
-                sums = lax.fori_loop(0, n, update_piece, sums, unroll=2 if n % 2 == 0 else 1)
+                sums = lax.fori_loop(0, n, update_piece, sums, unroll=2 if n % 2 == 0 else (n if n < 4 else 1))
 
     n_layer = decay_ref.shape[0]
     lane = lax.broadcasted_iota(jnp.int32, (1, LANES), 1)
-    lines = []
-    for b in range(blocks):
-        chosen = jnp.where(lives[b] > 0, layers[b], -LANES)
-        for q, values in enumerate((sums[1], sums[0])):
+
+    def by_layer(values):
+        terms = []
+        for b in range(blocks):
+            chosen = jnp.where(lives[b] > 0, layers[b], -LANES)
             block = values[b * block_rows : (b + 1) * block_rows]
-            lines.append(jnp.where(lane == chosen + q * n_layer, jnp.sum(block, axis=1, keepdims=True), 0.0))
-    line = jnp.sum(sum(lines[1:], lines[0]), axis=0, keepdims=True)
+            terms.append(jnp.where(lane == chosen, jnp.sum(block, axis=1, keepdims=True), 0.0))
+        return jnp.sum(sum(terms[1:], terms[0]), axis=0, keepdims=True)
+
+    line = (by_layer(sums[1]), by_layer(sums[0]))
 
     def all_sum(line, slots, send_sem, recv_sem, index, peers):
-        slots[index] = line
+        for q in range(2):
+            slots[index, q] = line[q]
         for peer in peers:
             pltpu.make_async_remote_copy(
                 src_ref=slots.at[index], dst_ref=slots.at[index],
@@ -344,16 +444,19 @@
         )
         with jax.named_scope("allw"):
             both.wait_recv()
-        terms = [slots[j] for j in range(len(peers) + 1)]
-        while len(terms) > 1:
-            terms = [sum(terms[i + 1 : i + 2], terms[i]) for i in range(0, len(terms), 2)]
-        return terms[0], both
+
+        def total(q):
+            terms = [slots[j, q] for j in range(len(peers) + 1)]
+            while len(terms) > 1:
+                terms = [sum(terms[i + 1 : i + 2], terms[i]) for i in range(0, len(terms), 2)]
+            return terms[0]
+
+        return (total(0), total(1)), both
 
     if one_shot:
         every = [
-            (lax.rem(sec + i, n_sec), lax.rem(me + j, n_shard))
-            for i in (*range(1, n_sec), 0) for j in range(n_shard) if i or j
-        ]
+            (i + jnp.where(i >= sec, 1, 0), j) for i in range(n_sec - 1) for j in range(n_shard)
+        ] + [(sec, lax.rem(me + j, n_shard)) for j in range(1, n_shard)]
         line, sent = all_sum(line, tiles, t_send, t_recv, sec * n_shard + me, every)
         sends = [sent]
     else:
@@ -362,7 +465,7 @@
         line, sent = all_sum(line, tiles, t_send, t_recv, me, shard_peers)
         line, zsent = all_sum(line, ztiles, z_send, z_recv, sec, sec_peers)
         sends = [sent, zsent]
-    ratios = jnp.sqrt(line / (pltpu.roll(line, LANES - n_layer, 1) + 1.0))
+    ratios = jnp.sqrt(line[0] / (line[1] + 1.0))
     ratio_ref[...] = ratios[0, :n_layer]
     step_ref[...] = jnp.concatenate(
         [
@@ -377,7 +480,7 @@
         axis=0,
     )
     with jax.named_scope("endw"):
-        for group in (*ones.values(), *twos.values(), sends):
+        for group in (*(ones[k, d] for k in range(count) if k != SHIFT for d in range(2)), *twos.values(), sends):
             for c in group:
                 c.wait_send()
 
@@ -385,11 +488,13 @@
 def finish(parts, p_v, upd, new1_v, new2_v, step_v, ratio_v, newp_hbm, new1_hbm, new2_hbm, ratio_hbm, newp_v, sem):
     cols = p_v.shape[1]
     width = cols // parts
-    copies = []
-    for i, (src, dst) in enumerate(((ratio_v, ratio_hbm), (new1_v, new1_hbm), (new2_v, new2_hbm))):
-        c = pltpu.make_async_copy(src, dst, sem.at[i])
+    copies = [pltpu.make_async_copy(ratio_v, ratio_hbm, sem.at[0])]
+    for k in range(parts):
+        span = pl.ds(k * width, width)
+        for i, (src, dst) in enumerate(((new1_v, new1_hbm), (new2_v, new2_hbm))):
+            copies.append(pltpu.make_async_copy(src.at[:, span], dst.at[:, span], sem.at[1 + i * parts + k]))
+    for c in copies:
         c.start()
-        copies.append(c)
     row_step = step_v[...]
 
     for k in range(parts):
@@ -401,7 +506,7 @@
 
         lax.fori_loop(0, width // LANES, step_piece, 0, unroll=4)
         span = pl.ds(k * width, width)
-        c = pltpu.make_async_copy(newp_v.at[:, span], newp_hbm.at[:, span], sem.at[3 + k])
+        c = pltpu.make_async_copy(newp_v.at[:, span], newp_hbm.at[:, span], sem.at[1 + 2 * parts + k])
         c.start()
         copies.append(c)
     for c in copies:
@@ -417,12 +522,10 @@
     n_layer = decay.shape[0]
     half = cols // 2
     cuts = tuple(half // LANES * c // CUTS[-1] * LANES for c in CUTS)
-    count = len(cuts)
     bf16, f32 = jnp.bfloat16, jnp.float32
     dma = pltpu.SemaphoreType.DMA
     one_shot = ONE_SHOT and n_shard * n_sec <= 32
     n_lines = n_shard * n_sec if one_shot else n_shard
-    most = max(n_x, n_y) - 1
     grads = grad_parts.reshape(n_y, n_x, 2, rows, cols)
     any_spec = pl.BlockSpec(memory_space=pltpu.HBM)
     vmem = pl.BlockSpec(memory_space=pltpu.VMEM)
@@ -451,18 +554,13 @@
             pltpu.VMEM((n_x - 1, rows, half), bf16),
             pltpu.VMEM((n_x - 1, n_y, rows, cuts[0]), bf16),
             pltpu.VMEM((n_y - 1, n_x, rows, cuts[0]), bf16),
-            pltpu.VMEM((n_lines, 1, LANES), f32),
-            None if one_shot else pltpu.VMEM((n_sec, 1, LANES), f32),
+            pltpu.VMEM((n_x - 1, n_y, rows, cuts[SHIFT] - cuts[SHIFT - 1]), bf16),
+            pltpu.VMEM((n_y - 1, n_x, rows, cuts[SHIFT] - cuts[SHIFT - 1]), bf16),
+            pltpu.VMEM((n_lines, 2, 1, LANES), f32),
+            None if one_shot else pltpu.VMEM((n_sec, 2, 1, LANES), f32),
             pltpu.SMEM(block_layer.shape, jnp.int32),
             pltpu.SMEM(block_valid.shape, jnp.int32),
             pltpu.SMEM(decay.shape, f32),
-            dma((count, 2)),
-            dma((count, 2, most)),
-            dma((count, 2, most)),
-            dma((2, most)),
-            dma((1,)),
-            dma((1,)),
-            pltpu.SemaphoreType.REGULAR((2, n_sec - 1)),
         ],
         compiler_params=pltpu.CompilerParams(
             collective_id=0, has_side_effects=True, vmem_limit_bytes=56 * 1024 * 1024
@@ -478,7 +576,7 @@
         ),
         in_specs=[vmem] * 6,
         out_specs=(any_spec,) * 4,
-        scratch_shapes=[pltpu.VMEM((rows, cols), bf16), dma((3 + PARTS,))],
+        scratch_shapes=[pltpu.VMEM((rows, cols), bf16), dma((1 + 3 * PARTS,))],
         compiler_params=pltpu.CompilerParams(vmem_limit_bytes=8 * 1024 * 1024),
     )(*held)
     return (out[0][None], out[1][None], out[2][None], out[3])

time: 32.7 us -> 31.4 us (0.960)
  Pallas kernels: 31.9 us -> 30.6 us
    pallas_call x1, Pallas kernels: 30.3 us -> 29 us  [shards(): pl.pallas_call(functools.partial(kernel, n_sec, n_y, n_x, cuts), out_shap...]
where the time goes in v2:
time: 31.4 us; the launch traced here: 31.3 us
  Pallas kernels  30.6 us (97%)
  between operations  0.64 us (2%)
    pallas_call x1, Pallas kernels, shards(): pl.pallas_call(functools.partial(kernel, n_sec, n_y, n_x, cuts), out_shap...  29 us
    pallas_call x1, Pallas kernels, shards(): pl.pallas_call(functools.partial(finish, PARTS), out_shape=(jax.ShapeDtyp...  1.59 us

profile of v2, /device:TPU:0, one launch (start us, length us, event | category | flops | bytes accessed | tf_op | source)
XLA Modules:
  0.0 31.3 jit_solution(8855279933174001465)
XLA Ops:
  0.6 29.0 %shard_map.102 = (bf16[32,8192]{1,0:T(8,128)(2,1)S(1)}, f32[32,8192]{1,0:T(8,128)S(1)}, f32[32,8192]{1,0:T(8,128)S(1)}, f32[32,8192]{1,0:T(8,128)S(1)}, f32[32,128]{1,0:T(8,128)S(1)}, /*index=5*/f32[8]{0:T(128)S(1)}) custom-call(bf16[2,2,2,32,8192]{4,3,2,1,0:T(8,128)(2,1)} %bitcast.7, bf16[32,8192]{1,0:T(8,128)(2,1)} %bitcast.10, f32[32,8192]{1,0:T(8,128)} %bitcast.8, ...), custom_call_target="tpu_custom_call" | custom-call | tf_op jit(solution)/shard_map/pallas_call | solution.py:532
  29.7 1.6 %shard_map.103 = (bf16[32,8192]{1,0:T(8,128)(2,1)}, f32[32,8192]{1,0:T(8,128)}, f32[32,8192]{1,0:T(8,128)}, f32[8]{0:T(128)}) custom-call(bf16[32,8192]{1,0:T(8,128)(2,1)S(1)} %get-tuple-element.14.p_v, f32[32,8192]{1,0:T(8,128)S(1)} %get-tuple-element.15.upd, f32[32,8192]{1,0:T(8,128)S(1)} %get-tuple-element.16.new1_v, ...), custom_call_target="tpu_custom_call" | custom-call | tf_op jit(solution)/shard_map/pallas_call | solution.py:569

commit v3 on v2

--- a/solution.py
+++ b/solution.py
@@ -13,10 +13,10 @@
 bias_second = 1.0 - 0.99**10
 root_second = math.sqrt(bias_second)
 LANES = 128
-CUTS = (2, 4, 7, 15, 23, 29, 31, 32)
+CUTS = (2, 4, 7, 13, 21, 27, 30, 31, 32)
 SHIFT = 2
 ONE_SHOT = True
-PARTS = 4
+PARTS = 2
 
 
 def kernel(
@@ -54,6 +54,7 @@
         t_recv=dma((1,)),
         z_recv=dma((1,)),
         told=pltpu.SemaphoreType.REGULAR((2, n_sec - 1)),
+        inside=pltpu.SemaphoreType.REGULAR,
     )
 
 
@@ -63,7 +64,7 @@
     p_v, upd, new1_ref, new2_ref, step_ref, ratio_ref,
     mine, d2d, m1_v, m2_v, r1, s1, r2, other, lent, tiles, ztiles, layer_ref, valid_ref, decay_ref,
     load_sem, state_sem, pair_send, one_send, two_send, raw_send, lent_send, lent_recv, t_send, z_send,
-    pair_recv, one_recv, two_recv, raw_recv, t_recv, z_recv, told,
+    pair_recv, one_recv, two_recv, raw_recv, t_recv, z_recv, told, inside,
 ):
     rows, cols = p_v.shape
     half = cols // 2
@@ -71,6 +72,7 @@
     n_shard = 2 * n_y * n_x
     sec, me = lax.axis_index("section"), lax.axis_index("shard")
     core = lax.rem(me, 2)
+    is_far, is_near = core == 0, core == 1
     x = lax.rem(me // 2, n_x)
     y = me // (2 * n_x)
     blocks = layer_ref.shape[1]
@@ -97,11 +99,10 @@
             loads[k, d] = c
         if k == 0:
             barrier = pltpu.get_barrier_semaphore()
-            near = [at(y, x, 1 - core)]
-            for cc in (core, 1 - core):
-                near += [at(y, lax.rem(x + j, n_x), cc) for j in range(1, n_x)]
-                near += [at(lax.rem(y + j, n_y), x, cc) for j in range(1, n_y)]
-            for peer in near:
+            beside = at(y, x, 1 - core)
+            around = [at(y, lax.rem(x + j, n_x), 1) for j in range(1, n_x)]
+            around += [at(lax.rem(y + j, n_y), x, 1) for j in range(1, n_y)]
+            for peer in around:
                 pl.semaphore_signal(barrier, inc=1, device_id=peer, device_id_type=MESH)
             last_sec = n_sec - 1
             up = (jnp.minimum(sec + 1, last_sec), me)
@@ -109,11 +110,15 @@
 
             @pl.when(sec < last_sec)
             def _():
-                pl.semaphore_signal(barrier, inc=1, device_id=up, device_id_type=MESH)
+                pl.semaphore_signal(barrier, inc=1, device_id=(up[0], me - core + 1), device_id_type=MESH)
 
             @pl.when(sec > 0)
             def _():
-                pl.semaphore_signal(barrier, inc=1, device_id=down, device_id_type=MESH)
+                pl.semaphore_signal(barrier, inc=1, device_id=(down[0], me - core + 1), device_id_type=MESH)
+
+            @pl.when(is_near)
+            def _():
+                pl.semaphore_signal(barrier, inc=1, device_id=beside, device_id_type=MESH)
 
     states = [
         pltpu.make_async_copy(src, dst, state_sem.at[i])
@@ -128,8 +133,27 @@
         s.start()
 
     ends = jnp.where(sec < last_sec, 1, 0) + jnp.where(sec > 0, 1, 0)
-    with jax.named_scope("bar"):
-        pl.semaphore_wait(barrier, len(near) + ends)
+
+    @pl.when(is_far)
+    def _():
+        pl.semaphore_wait(barrier, 1)
+        pl.semaphore_signal(inside, inc=1, device_id=beside, device_id_type=MESH)
+
+    @pl.when(is_near)
+    def _():
+        pl.semaphore_wait(inside, 1)
+
+    def meet():
+        with jax.named_scope("bar"):
+
+            @pl.when(is_near)
+            def _():
+                pl.semaphore_wait(barrier, 2 * (len(around) + ends))
+                pl.semaphore_signal(inside, inc=1, device_id=beside, device_id_type=MESH)
+
+            @pl.when(is_far)
+            def _():
+                pl.semaphore_wait(inside, 1)
 
     def relay(d):
         if 1 < d <= n_sec:
@@ -218,23 +242,19 @@
             )
             for j, t in others(d)
         ]
-    is_far, is_near = core == 0, core == 1
-
-    for d in range(2):
-        with jax.named_scope(f"ldw0{d}"):
-            loads[0, d].wait()
+
+    def send_raw(d):
         for c in ones[0, d]:
             c.start()
 
         @pl.when(is_near)
-        def _(d=d):
+        def _():
             for c in raws[d]:
                 c.start()
 
     def send_pair(k, d):
-        if k:
-            with jax.named_scope(f"ldw{k}{d}"):
-                loads[k, d].wait()
+        with jax.named_scope(f"ldw{k}{d}"):
+            loads[k, d].wait()
         if k in (0, SHIFT):
 
             @pl.when(is_far)
@@ -310,9 +330,13 @@
             for c in ones[k, d]:
                 c.start()
 
-    ahead = 4
+    ahead = 3
     order = [1, 0, *range(2, count)]
-    for k in order[: 1 + ahead]:
+    for i, k in enumerate(order[: 1 + ahead]):
+        if i == 2:
+            meet()
+            for d in range(2):
+                send_raw(d)
         for d in range(2):
             send_pair(k, d)
     for i, k in enumerate(order):
@@ -330,6 +354,33 @@
             if k == 0:
                 total += other[d][i, t, :, raw_cut].astype(jnp.float32)
         return total
+
+    def by_block(scalars):
+        return jnp.concatenate([jnp.full((block_rows, LANES), s) for s in scalars], axis=0)
+
+    for s in states:
+        s.wait()
+    layers = [layer_ref[0, b] for b in range(blocks)]
+    lives = [valid_ref[0, b] for b in range(blocks)]
+    row_decay = by_block([decay_ref[layer] for layer in layers])
+    row_live = by_block([jnp.where(v > 0, 1.0, 0.0).astype(jnp.float32) for v in lives]) > 0.5
+    n_layer = decay_ref.shape[0]
+    lane = lax.broadcasted_iota(jnp.int32, (1, LANES), 1)
+
+    def by_layer(values, offset):
+        terms = []
+        for b in range(blocks):
+            chosen = jnp.where(lives[b] > 0, layers[b] + offset, -1)
+            block = values[b * block_rows : (b + 1) * block_rows]
+            terms.append(jnp.where(lane == chosen, jnp.sum(block, axis=1, keepdims=True), 0.0))
+        return jnp.sum(sum(terms[1:], terms[0]), axis=0, keepdims=True)
+
+    def weigh(i, wsum):
+        weights = p_v[:, pl.ds(pl.multiple_of(i * LANES, LANES), LANES)].astype(jnp.float32)
+        return wsum + weights * weights
+
+    zero = jnp.zeros((rows, LANES), jnp.float32)
+    weight_line = by_layer(lax.fori_loop(0, cols // LANES, weigh, zero, unroll=2), 0)
 
     twos = {}
     for k in range(count):
@@ -359,15 +410,6 @@
     for k in range(count, n_sec):
         relay(k + 1)
 
-    def by_block(scalars):
-        return jnp.concatenate([jnp.full((block_rows, LANES), s) for s in scalars], axis=0)
-
-    for s in states:
-        s.wait()
-    layers = [layer_ref[0, b] for b in range(blocks)]
-    lives = [valid_ref[0, b] for b in range(blocks)]
-    row_decay = by_block([decay_ref[layer] for layer in layers])
-    row_live = by_block([jnp.where(v > 0, 1.0, 0.0).astype(jnp.float32) for v in lives]) > 0.5
     for d in range(2):
         for k in range(count):
             if k not in (0, SHIFT):
@@ -383,16 +425,14 @@
             for c in (pair[0, d], pair[SHIFT, d], *lends[d]):
                 c.wait_send()
 
-    zero = jnp.zeros((rows, LANES), jnp.float32)
-    sums = (zero, zero)
+    usum = zero
     for k in range(count):
         for d in range(2):
             with jax.named_scope(f"twow{k}{d}"):
                 for c in twos[k, d]:
                     c.wait_recv()
 
-            def update_piece(i, sums, k=k, d=d):
-                usum, wsum = sums
+            def update_piece(i, usum, k=k, d=d):
                 raw_cut = pl.ds(pl.multiple_of(i * LANES, LANES), LANES)
                 near_cut = pl.ds(pl.multiple_of(starts[k] + i * LANES, LANES), LANES)
                 cut = pl.ds(pl.multiple_of(d * half + starts[k] + i * LANES, LANES), LANES)
@@ -409,28 +449,16 @@
                 upd[:, cut] = update
                 new1_ref[:, cut] = jnp.where(row_live, first, old1)
                 new2_ref[:, cut] = jnp.where(row_live, second, old2)
-                return usum + update * update, wsum + weights * weights
+                return usum + update * update
 
             n = (cuts[k] - starts[k]) // LANES
             with jax.named_scope(f"upd{k}{d}"):
-                sums = lax.fori_loop(0, n, update_piece, sums, unroll=2 if n % 2 == 0 else (n if n < 4 else 1))
-
-    n_layer = decay_ref.shape[0]
-    lane = lax.broadcasted_iota(jnp.int32, (1, LANES), 1)
-
-    def by_layer(values):
-        terms = []
-        for b in range(blocks):
-            chosen = jnp.where(lives[b] > 0, layers[b], -LANES)
-            block = values[b * block_rows : (b + 1) * block_rows]
-            terms.append(jnp.where(lane == chosen, jnp.sum(block, axis=1, keepdims=True), 0.0))
-        return jnp.sum(sum(terms[1:], terms[0]), axis=0, keepdims=True)
-
-    line = (by_layer(sums[1]), by_layer(sums[0]))
-
-    def all_sum(line, slots, send_sem, recv_sem, index, peers):
-        for q in range(2):
-            slots[index, q] = line[q]
+                usum = lax.fori_loop(0, n, update_piece, usum, unroll=2 if n % 2 == 0 else (n if n < 4 else 1))
+
+    line = weight_line + by_layer(usum, n_layer)
+
+    def all_sum(line, slots, send_sem, recv_sem, index, peers, sent):
+        slots[index] = line
         for peer in peers:
             pltpu.make_async_remote_copy(
                 src_ref=slots.at[index], dst_ref=slots.at[index],
@@ -442,30 +470,32 @@
             src_ref=whole, dst_ref=whole, send_sem=send_sem.at[0], recv_sem=recv_sem.at[0],
             device_id=peers[0], device_id_type=MESH,
         )
+        if sent:
+            with jax.named_scope("endw"):
+                for c in sent:
+                    c.wait_send()
         with jax.named_scope("allw"):
             both.wait_recv()
-
-        def total(q):
-            terms = [slots[j, q] for j in range(len(peers) + 1)]
-            while len(terms) > 1:
-                terms = [sum(terms[i + 1 : i + 2], terms[i]) for i in range(0, len(terms), 2)]
-            return terms[0]
-
-        return (total(0), total(1)), both
-
+        terms = [slots[j] for j in range(len(peers) + 1)]
+        while len(terms) > 1:
+            terms = [sum(terms[i + 1 : i + 2], terms[i]) for i in range(0, len(terms), 2)]
+        return terms[0], both
+
+    groups = (*(ones[k, d] for k in range(count) if k != SHIFT for d in range(2)), *twos.values())
+    sent = [c for group in groups for c in group]
     if one_shot:
         every = [
             (i + jnp.where(i >= sec, 1, 0), j) for i in range(n_sec - 1) for j in range(n_shard)
         ] + [(sec, lax.rem(me + j, n_shard)) for j in range(1, n_shard)]
-        line, sent = all_sum(line, tiles, t_send, t_recv, sec * n_shard + me, every)
-        sends = [sent]
+        line, last = all_sum(line, tiles, t_send, t_recv, sec * n_shard + me, every, sent)
+        sends = [last]
     else:
         shard_peers = [(sec, lax.rem(me + j, n_shard)) for j in range(1, n_shard)]
         sec_peers = [(lax.rem(sec + j, n_sec), me) for j in range(1, n_sec)]
-        line, sent = all_sum(line, tiles, t_send, t_recv, me, shard_peers)
-        line, zsent = all_sum(line, ztiles, z_send, z_recv, sec, sec_peers)
-        sends = [sent, zsent]
-    ratios = jnp.sqrt(line[0] / (line[1] + 1.0))
+        line, last = all_sum(line, tiles, t_send, t_recv, me, shard_peers, sent)
+        line, zlast = all_sum(line, ztiles, z_send, z_recv, sec, sec_peers, [])
+        sends = [last, zlast]
+    ratios = jnp.sqrt(line / (pltpu.roll(line, LANES - n_layer, 1) + 1.0))
     ratio_ref[...] = ratios[0, :n_layer]
     step_ref[...] = jnp.concatenate(
         [
@@ -479,10 +509,8 @@
         ],
         axis=0,
     )
-    with jax.named_scope("endw"):
-        for group in (*(ones[k, d] for k in range(count) if k != SHIFT for d in range(2)), *twos.values(), sends):
-            for c in group:
-                c.wait_send()
+    for c in sends:
+        c.wait_send()
 
 
 def finish(parts, p_v, upd, new1_v, new2_v, step_v, ratio_v, newp_hbm, new1_hbm, new2_hbm, ratio_hbm, newp_v, sem):
@@ -556,8 +584,8 @@
             pltpu.VMEM((n_y - 1, n_x, rows, cuts[0]), bf16),
             pltpu.VMEM((n_x - 1, n_y, rows, cuts[SHIFT] - cuts[SHIFT - 1]), bf16),
             pltpu.VMEM((n_y - 1, n_x, rows, cuts[SHIFT] - cuts[SHIFT - 1]), bf16),
-            pltpu.VMEM((n_lines, 2, 1, LANES), f32),
-            None if one_shot else pltpu.VMEM((n_sec, 2, 1, LANES), f32),
+            pltpu.VMEM((n_lines, 1, LANES), f32),
+            None if one_shot else pltpu.VMEM((n_sec, 1, LANES), f32),
             pltpu.SMEM(block_layer.shape, jnp.int32),
             pltpu.SMEM(block_valid.shape, jnp.int32),
             pltpu.SMEM(decay.shape, f32),

time: 31.4 us -> 31 us (0.987)
  Pallas kernels: 30.6 us -> 30.2 us
    pallas_call x1, Pallas kernels: 29 us -> 28.6 us  [shards(): pl.pallas_call(functools.partial(kernel, n_sec, n_y, n_x, cuts), out_shap...]
where the time goes in v3:
time: 31 us; the launch traced here: 30.8 us
  Pallas kernels  30.2 us (97%)
  between operations  0.63 us (2%)
    pallas_call x1, Pallas kernels, shards(): pl.pallas_call(functools.partial(kernel, n_sec, n_y, n_x, cuts), out_shap...  28.6 us
    pallas_call x1, Pallas kernels, shards(): pl.pallas_call(functools.partial(finish, PARTS), out_shape=(jax.ShapeDtyp...  1.56 us

profile of v3, /device:TPU:0, one launch (start us, length us, event | category | flops | bytes accessed | tf_op | source)
XLA Modules:
  0.0 30.8 jit_solution(12843951759246875115)
XLA Ops:
  0.6 28.6 %shard_map.102 = (bf16[32,8192]{1,0:T(8,128)(2,1)S(1)}, f32[32,8192]{1,0:T(8,128)S(1)}, f32[32,8192]{1,0:T(8,128)S(1)}, f32[32,8192]{1,0:T(8,128)S(1)}, f32[32,128]{1,0:T(8,128)S(1)}, /*index=5*/f32[8]{0:T(128)S(1)}) custom-call(bf16[2,2,2,32,8192]{4,3,2,1,0:T(8,128)(2,1)} %bitcast.7, bf16[32,8192]{1,0:T(8,128)(2,1)} %bitcast.10, f32[32,8192]{1,0:T(8,128)} %bitcast.8, ...), custom_call_target="tpu_custom_call" | custom-call | tf_op jit(solution)/shard_map/pallas_call | solution.py:560
  29.3 1.6 %shard_map.103 = (bf16[32,8192]{1,0:T(8,128)(2,1)}, f32[32,8192]{1,0:T(8,128)}, f32[32,8192]{1,0:T(8,128)}, f32[8]{0:T(128)}) custom-call(bf16[32,8192]{1,0:T(8,128)(2,1)S(1)} %get-tuple-element.14.p_v, f32[32,8192]{1,0:T(8,128)S(1)} %get-tuple-element.15.upd, f32[32,8192]{1,0:T(8,128)S(1)} %get-tuple-element.16.new1_v, ...), custom_call_target="tpu_custom_call" | custom-call | tf_op jit(solution)/shard_map/pallas_call | solution.py:597

commit v4 on v3

--- a/solution.py
+++ b/solution.py
@@ -13,10 +13,11 @@
 bias_second = 1.0 - 0.99**10
 root_second = math.sqrt(bias_second)
 LANES = 128
-CUTS = (2, 4, 7, 13, 21, 27, 30, 31, 32)
+CUTS = (3, 5, 9, 17, 24, 28, 31, 32)
 SHIFT = 2
 ONE_SHOT = True
 PARTS = 2
+WIDE = 4
 
 
 def kernel(
@@ -42,7 +43,7 @@
         pair_send=dma((count, 2)),
         one_send=dma((count, 2, most)),
         two_send=dma((count, 2, most)),
-        raw_send=dma((2, 2, most)),
+        raw_send=dma((2, most)),
         lent_send=dma((2, 2, most)),
         lent_recv=dma((2, most)),
         t_send=dma((1,)),
@@ -55,6 +56,8 @@
         z_recv=dma((1,)),
         told=pltpu.SemaphoreType.REGULAR((2, n_sec - 1)),
         inside=pltpu.SemaphoreType.REGULAR,
+        whole=pltpu.SemaphoreType.REGULAR,
+        settled=pltpu.SemaphoreType.REGULAR,
     )
 
 
@@ -64,7 +67,7 @@
     p_v, upd, new1_ref, new2_ref, step_ref, ratio_ref,
     mine, d2d, m1_v, m2_v, r1, s1, r2, other, lent, tiles, ztiles, layer_ref, valid_ref, decay_ref,
     load_sem, state_sem, pair_send, one_send, two_send, raw_send, lent_send, lent_recv, t_send, z_send,
-    pair_recv, one_recv, two_recv, raw_recv, t_recv, z_recv, told, inside,
+    pair_recv, one_recv, two_recv, raw_recv, t_recv, z_recv, told, inside, whole, settled,
 ):
     rows, cols = p_v.shape
     half = cols // 2
@@ -100,24 +103,28 @@
         if k == 0:
             barrier = pltpu.get_barrier_semaphore()
             beside = at(y, x, 1 - core)
-            around = [at(y, lax.rem(x + j, n_x), 1) for j in range(1, n_x)]
-            around += [at(lax.rem(y + j, n_y), x, 1) for j in range(1, n_y)]
-            for peer in around:
-                pl.semaphore_signal(barrier, inc=1, device_id=peer, device_id_type=MESH)
+            around = [at(y, lax.rem(x + j, n_x), core) for j in range(1, n_x)]
+            around += [at(lax.rem(y + j, n_y), x, core) for j in range(1, n_y)]
             last_sec = n_sec - 1
             up = (jnp.minimum(sec + 1, last_sec), me)
             down = (jnp.maximum(sec - 1, 0), me)
-
-            @pl.when(sec < last_sec)
-            def _():
-                pl.semaphore_signal(barrier, inc=1, device_id=(up[0], me - core + 1), device_id_type=MESH)
-
-            @pl.when(sec > 0)
-            def _():
-                pl.semaphore_signal(barrier, inc=1, device_id=(down[0], me - core + 1), device_id_type=MESH)
+            ends = jnp.where(sec < last_sec, 1, 0) + jnp.where(sec > 0, 1, 0)
+
+            def tell(semaphore):
+                for peer in around:
+                    pl.semaphore_signal(semaphore, inc=1, device_id=peer, device_id_type=MESH)
+
+                @pl.when(sec < last_sec)
+                def _():
+                    pl.semaphore_signal(semaphore, inc=1, device_id=up, device_id_type=MESH)
+
+                @pl.when(sec > 0)
+                def _():
+                    pl.semaphore_signal(semaphore, inc=1, device_id=down, device_id_type=MESH)
 
             @pl.when(is_near)
             def _():
+                tell(barrier)
                 pl.semaphore_signal(barrier, inc=1, device_id=beside, device_id_type=MESH)
 
     states = [
@@ -132,28 +139,32 @@
     for s in states:
         s.start()
 
-    ends = jnp.where(sec < last_sec, 1, 0) + jnp.where(sec > 0, 1, 0)
-
     @pl.when(is_far)
     def _():
         pl.semaphore_wait(barrier, 1)
         pl.semaphore_signal(inside, inc=1, device_id=beside, device_id_type=MESH)
+        for d in range(2):
+            other[d][...] = jnp.zeros_like(other[d])
 
     @pl.when(is_near)
     def _():
-        pl.semaphore_wait(inside, 1)
+        with jax.named_scope("bar1"):
+            pl.semaphore_wait(inside, 1)
+            pl.semaphore_wait(barrier, len(around) + ends)
+        tell(whole)
+        pl.semaphore_signal(inside, inc=1, device_id=beside, device_id_type=MESH)
 
     def meet():
         with jax.named_scope("bar"):
 
             @pl.when(is_near)
             def _():
-                pl.semaphore_wait(barrier, 2 * (len(around) + ends))
-                pl.semaphore_signal(inside, inc=1, device_id=beside, device_id_type=MESH)
+                pl.semaphore_wait(whole, len(around) + ends)
+                pl.semaphore_signal(settled, inc=1, device_id=beside, device_id_type=MESH)
 
             @pl.when(is_far)
             def _():
-                pl.semaphore_wait(inside, 1)
+                pl.semaphore_wait(settled, 1)
 
     def relay(d):
         if 1 < d <= n_sec:
@@ -196,7 +207,7 @@
     def rows_of(d, t, cc, k):
         return mine.at[(*place(d, t), cc, slice(None), span(k, d))]
 
-    ones, raws, forwards, lends, crosses, pair, kept = {}, {}, {}, {}, {}, {}, {}
+    ones, raws, lends, crosses, pair, kept = {}, {}, {}, {}, {}, {}
     for d in range(2):
         for k in range(count):
             ones[k, d] = [
@@ -217,14 +228,7 @@
         raws[d] = [
             remote(
                 rows_of(d, t, 1 - core, 0), other[d].at[j - 1],
-                raw_send.at[0, d, j - 1], raw_recv.at[d, j - 1], peer_at(d, t, 1 - core),
-            )
-            for j, t in others(d)
-        ]
-        forwards[d] = [
-            remote(
-                d2d.at[(*place(d, t), slice(None), span(0, d))], other[d].at[j - 1],
-                raw_send.at[1, d, j - 1], raw_recv.at[d, j - 1], peer_at(d, t, core),
+                raw_send.at[d, j - 1], raw_recv.at[d, j - 1], peer_at(d, t, 1 - core),
             )
             for j, t in others(d)
         ]
@@ -243,26 +247,25 @@
             for j, t in others(d)
         ]
 
-    def send_raw(d):
-        for c in ones[0, d]:
-            c.start()
-
-        @pl.when(is_near)
-        def _():
-            for c in raws[d]:
-                c.start()
-
     def send_pair(k, d):
-        with jax.named_scope(f"ldw{k}{d}"):
-            loads[k, d].wait()
-        if k in (0, SHIFT):
+        if k:
+            with jax.named_scope(f"ldw{k}{d}"):
+                loads[k, d].wait()
+        if k == 0:
 
             @pl.when(is_far)
             def _():
+                kept[k, d].start()
+
+            @pl.when(is_near)
+            def _():
                 pair[k, d].start()
-                if k:
-                    for c in lends[d]:
-                        c.start()
+        elif k == SHIFT:
+
+            @pl.when(is_far)
+            def _():
+                for c in (pair[k, d], *lends[d]):
+                    c.start()
 
             @pl.when(is_near)
             def _():
@@ -291,15 +294,16 @@
 
             @pl.when(is_near)
             def _():
+                kept[k, d].wait_recv()
+                add_kept(d, cut)
+
+            @pl.when(is_far)
+            def _():
                 pair[k, d].wait_recv()
-                for c in forwards[d]:
+                add_all(cut)
+                for c in ones[k, d]:
                     c.start()
 
-            @pl.when(is_far)
-            def _():
-                kept[k, d].wait_recv()
-
-            add_kept(d, cut)
         elif k == SHIFT:
 
             @pl.when(is_near)
@@ -330,13 +334,28 @@
             for c in ones[k, d]:
                 c.start()
 
+    for d in range(2):
+        with jax.named_scope(f"ldw0{d}"):
+            loads[0, d].wait()
+
+        @pl.when(is_near)
+        def _(d=d):
+            for c in ones[0, d]:
+                c.start()
+
     ahead = 3
     order = [1, 0, *range(2, count)]
     for i, k in enumerate(order[: 1 + ahead]):
         if i == 2:
+
+            @pl.when(is_far)
+            def _():
+                pl.semaphore_wait(inside, 1)
+                for d in range(2):
+                    for c in raws[d]:
+                        c.start()
+
             meet()
-            for d in range(2):
-                send_raw(d)
         for d in range(2):
             send_pair(k, d)
     for i, k in enumerate(order):
@@ -389,8 +408,12 @@
                 for c in ones[k, d]:
                     c.wait_recv()
                 if k == 0:
-                    for c in forwards[d]:
-                        c.wait_recv()
+
+                    @pl.when(is_near)
+                    def _(d=d):
+                        for c in raws[d]:
+                            c.wait_recv()
+
             group = []
             for j in range(1, second_n[d]):
                 at_hand = y if d == 0 else x
@@ -405,10 +428,10 @@
                 c.start()
                 group.append(c)
             twos[k, d] = group
-        if k < n_sec:
-            relay(k + 1)
-    for k in range(count, n_sec):
-        relay(k + 1)
+        if 0 < k <= n_sec:
+            relay(k)
+    for k in range(count, n_sec + 1):
+        relay(k)
 
     for d in range(2):
         for k in range(count):
@@ -417,13 +440,16 @@
 
         @pl.when(is_near)
         def _(d=d):
-            for c in (kept[0, d], kept[SHIFT, d], *raws[d], *forwards[d], *ones[SHIFT, d], *crosses[d]):
+            for c in (pair[0, d], kept[SHIFT, d], *ones[SHIFT, d], *crosses[d]):
                 c.wait_send()
 
         @pl.when(is_far)
         def _(d=d):
-            for c in (pair[0, d], pair[SHIFT, d], *lends[d]):
+            for c in (kept[0, d], pair[SHIFT, d], *lends[d], *raws[d]):
                 c.wait_send()
+
+    def lanes(start):
+        return pl.ds(start if isinstance(start, int) else pl.multiple_of(start, LANES), LANES)
 
     usum = zero
     for k in range(count):
@@ -433,9 +459,7 @@
                     c.wait_recv()
 
             def update_piece(i, usum, k=k, d=d):
-                raw_cut = pl.ds(pl.multiple_of(i * LANES, LANES), LANES)
-                near_cut = pl.ds(pl.multiple_of(starts[k] + i * LANES, LANES), LANES)
-                cut = pl.ds(pl.multiple_of(d * half + starts[k] + i * LANES, LANES), LANES)
+                raw_cut, near_cut, cut = (lanes(base + i * LANES) for base in (0, starts[k], d * half + starts[k]))
                 grad = partial(k, d, y if d == 0 else x, cut, near_cut, raw_cut)
                 for j in range(second_n[d] - 1):
                     grad += r2[d][j, :, near_cut].astype(jnp.float32)
@@ -452,8 +476,16 @@
                 return usum + update * update
 
             n = (cuts[k] - starts[k]) // LANES
+
+            def update_block(i, usum):
+                for u in range(WIDE):
+                    usum = update_piece(i * WIDE + u, usum)
+                return usum
+
             with jax.named_scope(f"upd{k}{d}"):
-                usum = lax.fori_loop(0, n, update_piece, usum, unroll=2 if n % 2 == 0 else (n if n < 4 else 1))
+                usum = lax.fori_loop(0, n // WIDE, update_block, usum)
+                for i in range(n // WIDE * WIDE, n):
+                    usum = update_piece(i, usum)
 
     line = weight_line + by_layer(usum, n_layer)
 

time: 31 us -> 30.6 us (0.987)
  Pallas kernels: 30.2 us -> 29.8 us
    pallas_call x1, Pallas kernels: 28.6 us -> 28.2 us  [shards(): pl.pallas_call(functools.partial(kernel, n_sec, n_y, n_x, cuts), out_shap...]
where the time goes in v4:
time: 30.6 us; the launch traced here: 30.4 us
  Pallas kernels  29.8 us (97%)
  between operations  0.63 us (2%)
    pallas_call x1, Pallas kernels, shards(): pl.pallas_call(functools.partial(kernel, n_sec, n_y, n_x, cuts), out_shap...  28.2 us
    pallas_call x1, Pallas kernels, shards(): pl.pallas_call(functools.partial(finish, PARTS), out_shape=(jax.ShapeDtyp...  1.56 us

profile of v4, /device:TPU:0, one launch (start us, length us, event | category | flops | bytes accessed | tf_op | source)
XLA Modules:
  0.0 30.4 jit_solution(14836625354919027296)
XLA Ops:
  0.6 28.2 %shard_map.102 = (bf16[32,8192]{1,0:T(8,128)(2,1)S(1)}, f32[32,8192]{1,0:T(8,128)S(1)}, f32[32,8192]{1,0:T(8,128)S(1)}, f32[32,8192]{1,0:T(8,128)S(1)}, f32[32,128]{1,0:T(8,128)S(1)}, /*index=5*/f32[8]{0:T(128)S(1)}) custom-call(bf16[2,2,2,32,8192]{4,3,2,1,0:T(8,128)(2,1)} %bitcast.7, bf16[32,8192]{1,0:T(8,128)(2,1)} %bitcast.10, f32[32,8192]{1,0:T(8,128)} %bitcast.8, ...), custom_call_target="tpu_custom_call" | custom-call | tf_op jit(solution)/shard_map/pallas_call | solution.py:592
  28.9 1.6 %shard_map.103 = (bf16[32,8192]{1,0:T(8,128)(2,1)}, f32[32,8192]{1,0:T(8,128)}, f32[32,8192]{1,0:T(8,128)}, f32[8]{0:T(128)}) custom-call(bf16[32,8192]{1,0:T(8,128)(2,1)S(1)} %get-tuple-element.14.p_v, f32[32,8192]{1,0:T(8,128)S(1)} %get-tuple-element.15.upd, f32[32,8192]{1,0:T(8,128)S(1)} %get-tuple-element.16.new1_v, ...), custom_call_target="tpu_custom_call" | custom-call | tf_op jit(solution)/shard_map/pallas_call | solution.py:629

commit v5 on v4

--- a/solution.py
+++ b/solution.py
@@ -23,7 +23,7 @@
 def kernel(
     n_sec, n_y, n_x, cuts,
     g_hbm, p_hbm, m1_hbm, m2_hbm, layer_hbm, valid_hbm, decay_hbm,
-    p_v, upd, new1_ref, new2_ref, step_ref, ratio_ref,
+    p_v, upd, new1_ref, new2_ref, chosen_ref, total_ref,
     mine, d2d, m1_v, m2_v, r1x, r1y, s1x, s1y, r2x, r2y, xa, ya, xs, ys, tiles, ztiles, layer_ref, valid_ref, decay_ref,
 ):
     count = len(cuts)
@@ -34,7 +34,7 @@
         functools.partial(
             body, n_sec, n_y, n_x, cuts, one_shot,
             g_hbm, p_hbm, m1_hbm, m2_hbm, layer_hbm, valid_hbm, decay_hbm,
-            p_v, upd, new1_ref, new2_ref, step_ref, ratio_ref,
+            p_v, upd, new1_ref, new2_ref, chosen_ref, total_ref,
             mine, d2d, m1_v, m2_v, (r1x, r1y), (s1x, s1y), (r2x, r2y), (xa, ya), (xs, ys), tiles, ztiles,
             layer_ref, valid_ref, decay_ref,
         ),
@@ -64,7 +64,7 @@
 def body(
     n_sec, n_y, n_x, cuts, one_shot,
     g_hbm, p_hbm, m1_hbm, m2_hbm, layer_hbm, valid_hbm, decay_hbm,
-    p_v, upd, new1_ref, new2_ref, step_ref, ratio_ref,
+    p_v, upd, new1_ref, new2_ref, chosen_ref, total_ref,
     mine, d2d, m1_v, m2_v, r1, s1, r2, other, lent, tiles, ztiles, layer_ref, valid_ref, decay_ref,
     load_sem, state_sem, pair_send, one_send, two_send, raw_send, lent_send, lent_recv, t_send, z_send,
     pair_recv, one_recv, two_recv, raw_recv, t_recv, z_recv, told, inside, whole, settled,
@@ -92,15 +92,16 @@
     def inner(k):
         return pl.ds(starts[k], cuts[k] - starts[k])
 
+    order = [1, 0, *range(2, count)]
     loads = {}
-    for k in range(count):
+    for k in order:
         for d in range(2):
             c = pltpu.make_async_copy(
                 g_hbm.at[:, :, :, :, span(k, d)], mine.at[:, :, :, :, span(k, d)], load_sem.at[k, d]
             )
             c.start()
             loads[k, d] = c
-        if k == 0:
+        if k == 1:
             barrier = pltpu.get_barrier_semaphore()
             beside = at(y, x, 1 - core)
             around = [at(y, lax.rem(x + j, n_x), core) for j in range(1, n_x)]
@@ -255,6 +256,7 @@
 
             @pl.when(is_far)
             def _():
+                loads[k, d].wait()
                 kept[k, d].start()
 
             @pl.when(is_near)
@@ -334,17 +336,14 @@
             for c in ones[k, d]:
                 c.start()
 
-    for d in range(2):
-        with jax.named_scope(f"ldw0{d}"):
+    @pl.when(is_near)
+    def _():
+        for d in range(2):
             loads[0, d].wait()
-
-        @pl.when(is_near)
-        def _(d=d):
             for c in ones[0, d]:
                 c.start()
 
     ahead = 3
-    order = [1, 0, *range(2, count)]
     for i, k in enumerate(order[: 1 + ahead]):
         if i == 2:
 
@@ -399,6 +398,13 @@
         return wsum + weights * weights
 
     zero = jnp.zeros((rows, LANES), jnp.float32)
+    chosen_ref[...] = jnp.concatenate(
+        [
+            jnp.broadcast_to(jnp.where((lane == layers[b]) & (lives[b] > 0), 0.1, 0.0), (block_rows, LANES))
+            for b in range(blocks)
+        ],
+        axis=0,
+    )
     weight_line = by_layer(lax.fori_loop(0, cols // LANES, weigh, zero, unroll=2), 0)
 
     twos = {}
@@ -527,35 +533,31 @@
         line, last = all_sum(line, tiles, t_send, t_recv, me, shard_peers, sent)
         line, zlast = all_sum(line, ztiles, z_send, z_recv, sec, sec_peers, [])
         sends = [last, zlast]
-    ratios = jnp.sqrt(line / (pltpu.roll(line, LANES - n_layer, 1) + 1.0))
-    ratio_ref[...] = ratios[0, :n_layer]
-    step_ref[...] = jnp.concatenate(
-        [
-            jnp.broadcast_to(
-                0.1 * jnp.sum(
-                    jnp.where((lane == layers[b]) & (lives[b] > 0), ratios, 0.0), axis=1, keepdims=True
-                ),
-                (block_rows, LANES),
-            )
-            for b in range(blocks)
-        ],
-        axis=0,
-    )
+    total_ref[...] = line
     for c in sends:
         c.wait_send()
 
 
-def finish(parts, p_v, upd, new1_v, new2_v, step_v, ratio_v, newp_hbm, new1_hbm, new2_hbm, ratio_hbm, newp_v, sem):
+def finish(
+    parts, p_v, upd, new1_v, new2_v, chosen_v, total_v, newp_hbm, new1_hbm, new2_hbm, ratio_hbm, newp_v, ratio_v, sem
+):
     cols = p_v.shape[1]
     width = cols // parts
-    copies = [pltpu.make_async_copy(ratio_v, ratio_hbm, sem.at[0])]
+    copies = []
     for k in range(parts):
         span = pl.ds(k * width, width)
         for i, (src, dst) in enumerate(((new1_v, new1_hbm), (new2_v, new2_hbm))):
             copies.append(pltpu.make_async_copy(src.at[:, span], dst.at[:, span], sem.at[1 + i * parts + k]))
     for c in copies:
         c.start()
-    row_step = step_v[...]
+    total = total_v[...]
+    n_layer = ratio_v.shape[0]
+    ratios = jnp.sqrt(total / (pltpu.roll(total, LANES - n_layer, 1) + 1.0))
+    ratios = jnp.where(lax.broadcasted_iota(jnp.int32, ratios.shape, 1) < n_layer, ratios, 0.0)
+    row_step = jnp.broadcast_to(jnp.sum(chosen_v[...] * ratios, axis=1, keepdims=True), chosen_v.shape)
+    ratio_v[...] = ratios[0, :n_layer]
+    copies.append(pltpu.make_async_copy(ratio_v, ratio_hbm, sem.at[0]))
+    copies[-1].start()
 
     for k in range(parts):
         def step_piece(i, carry, k=k):
@@ -597,7 +599,7 @@
             pltpu.VMEM((rows, cols), f32),
             pltpu.VMEM((rows, cols), f32),
             pltpu.VMEM((rows, LANES), f32),
-            pltpu.VMEM((n_layer,), f32),
+            pltpu.VMEM((1, LANES), f32),
         ),
         in_specs=[any_spec] * 7,
         out_specs=(vmem,) * 6,
@@ -636,7 +638,7 @@
         ),
         in_specs=[vmem] * 6,
         out_specs=(any_spec,) * 4,
-        scratch_shapes=[pltpu.VMEM((rows, cols), bf16), dma((1 + 3 * PARTS,))],
+        scratch_shapes=[pltpu.VMEM((rows, cols), bf16), pltpu.VMEM((n_layer,), f32), dma((1 + 3 * PARTS,))],
         compiler_params=pltpu.CompilerParams(vmem_limit_bytes=8 * 1024 * 1024),
     )(*held)
     return (out[0][None], out[1][None], out[2][None], out[3])

time: 30.6 us -> 30.4 us (level)
  no operation moved by 1% of the time
where the time goes in v5:
time: 30.4 us; the launch traced here: 30.2 us
  Pallas kernels  29.6 us (97%)
  between operations  0.63 us (2%)
    pallas_call x1, Pallas kernels, shards(): pl.pallas_call(functools.partial(kernel, n_sec, n_y, n_x, cuts), out_shap...  28 us
    pallas_call x1, Pallas kernels, shards(): pl.pallas_call(functools.partial(finish, PARTS), out_shape=(jax.ShapeDtyp...  1.55 us

profile of v5, /device:TPU:0, one launch (start us, length us, event | category | flops | bytes accessed | tf_op | source)
XLA Modules:
  0.0 30.2 jit_solution(5425638517299751348)
XLA Ops:
  0.6 28.0 %shard_map.102 = (bf16[32,8192]{1,0:T(8,128)(2,1)S(1)}, f32[32,8192]{1,0:T(8,128)S(1)}, f32[32,8192]{1,0:T(8,128)S(1)}, f32[32,8192]{1,0:T(8,128)S(1)}, f32[32,128]{1,0:T(8,128)S(1)}, /*index=5*/f32[1,128]{1,0:T(1,128)S(1)}) custom-call(bf16[2,2,2,32,8192]{4,3,2,1,0:T(8,128)(2,1)} %bitcast.7, bf16[32,8192]{1,0:T(8,128)(2,1)} %bitcast.10, ...), custom_call_target="tpu_custom_call" | custom-call | tf_op jit(solution)/shard_map/pallas_call | solution.py:594
  28.7 1.5 %shard_map.103 = (bf16[32,8192]{1,0:T(8,128)(2,1)}, f32[32,8192]{1,0:T(8,128)}, f32[32,8192]{1,0:T(8,128)}, f32[8]{0:T(128)}) custom-call(bf16[32,8192]{1,0:T(8,128)(2,1)S(1)} %get-tuple-element.14.p_v, f32[32,8192]{1,0:T(8,128)S(1)} %get-tuple-element.15.upd, f32[32,8192]{1,0:T(8,128)S(1)} %get-tuple-element.16.new1_v, ...), custom_call_target="tpu_custom_call" | custom-call | tf_op jit(solution)/shard_map/pallas_call | solution.py:631

commit v6 on v5

--- a/solution.py
+++ b/solution.py
@@ -13,7 +13,7 @@
 bias_second = 1.0 - 0.99**10
 root_second = math.sqrt(bias_second)
 LANES = 128
-CUTS = (3, 5, 9, 17, 24, 28, 31, 32)
+CUTS = (3, 5, 9, 17, 24, 29, 32)
 SHIFT = 2
 ONE_SHOT = True
 PARTS = 2

time: 30.4 us -> 30.4 us (level)
  no operation moved by 1% of the time
where the time goes in v6:
time: 30.4 us; the launch traced here: 30.2 us
  Pallas kernels  29.6 us (97%)
  between operations  0.63 us (2%)
    pallas_call x1, Pallas kernels, shards(): pl.pallas_call(functools.partial(kernel, n_sec, n_y, n_x, cuts), out_shap...  28.1 us
    pallas_call x1, Pallas kernels, shards(): pl.pallas_call(functools.partial(finish, PARTS), out_shape=(jax.ShapeDtyp...  1.55 us

profile of v6, /device:TPU:0, one launch (start us, length us, event | category | flops | bytes accessed | tf_op | source)
XLA Modules:
  0.0 30.2 jit_solution(8090004422170383193)
XLA Ops:
  0.6 28.1 %shard_map.102 = (bf16[32,8192]{1,0:T(8,128)(2,1)S(1)}, f32[32,8192]{1,0:T(8,128)S(1)}, f32[32,8192]{1,0:T(8,128)S(1)}, f32[32,8192]{1,0:T(8,128)S(1)}, f32[32,128]{1,0:T(8,128)S(1)}, /*index=5*/f32[1,128]{1,0:T(1,128)S(1)}) custom-call(bf16[2,2,2,32,8192]{4,3,2,1,0:T(8,128)(2,1)} %bitcast.7, bf16[32,8192]{1,0:T(8,128)(2,1)} %bitcast.10, ...), custom_call_target="tpu_custom_call" | custom-call | tf_op jit(solution)/shard_map/pallas_call | solution.py:594
  28.7 1.5 %shard_map.103 = (bf16[32,8192]{1,0:T(8,128)(2,1)}, f32[32,8192]{1,0:T(8,128)}, f32[32,8192]{1,0:T(8,128)}, f32[8]{0:T(128)}) custom-call(bf16[32,8192]{1,0:T(8,128)(2,1)S(1)} %get-tuple-element.14.p_v, f32[32,8192]{1,0:T(8,128)S(1)} %get-tuple-element.15.upd, f32[32,8192]{1,0:T(8,128)S(1)} %get-tuple-element.16.new1_v, ...), custom_call_target="tpu_custom_call" | custom-call | tf_op jit(solution)/shard_map/pallas_call | solution.py:631

commit v7 on v5

--- a/solution.py
+++ b/solution.py
@@ -343,8 +343,18 @@
             for c in ones[0, d]:
                 c.start()
 
-    ahead = 3
-    for i, k in enumerate(order[: 1 + ahead]):
+    ahead = 4
+    behind = 2
+
+    def push(which, i):
+        if 3 <= i < count:
+
+            @pl.when(which)
+            def _():
+                for d in range(2):
+                    send_pair(order[i], d)
+
+    for i, k in enumerate(order[:3]):
         if i == 2:
 
             @pl.when(is_far)
@@ -357,12 +367,15 @@
             meet()
         for d in range(2):
             send_pair(k, d)
+    for i in range(3, 1 + ahead):
+        push(is_near, i)
+    for i in range(3, 1 + behind):
+        push(is_far, i)
     for i, k in enumerate(order):
         for d in range(2):
             send_one(k, d)
-        if i + 1 + ahead < count:
-            for d in range(2):
-                send_pair(order[i + 1 + ahead], d)
+        push(is_near, i + 1 + ahead)
+        push(is_far, i + 1 + behind)
 
     def partial(k, d, t, cut, near_cut, raw_cut):
         yy, xx = (t, x) if d == 0 else (y, t)

time: 30.4 us -> 30.4 us (level)
  no operation moved by 1% of the time
where the time goes in v7:
time: 30.4 us; the launch traced here: 30.2 us
  Pallas kernels  29.6 us (97%)
  between operations  0.63 us (2%)
    pallas_call x1, Pallas kernels, shards(): pl.pallas_call(functools.partial(kernel, n_sec, n_y, n_x, cuts), out_shap...  28 us
    pallas_call x1, Pallas kernels, shards(): pl.pallas_call(functools.partial(finish, PARTS), out_shape=(jax.ShapeDtyp...  1.55 us

profile of v7, /device:TPU:0, one launch (start us, length us, event | category | flops | bytes accessed | tf_op | source)
XLA Modules:
  0.0 30.2 jit_solution(17962190249912416382)
XLA Ops:
  0.6 28.0 %shard_map.102 = (bf16[32,8192]{1,0:T(8,128)(2,1)S(1)}, f32[32,8192]{1,0:T(8,128)S(1)}, f32[32,8192]{1,0:T(8,128)S(1)}, f32[32,8192]{1,0:T(8,128)S(1)}, f32[32,128]{1,0:T(8,128)S(1)}, /*index=5*/f32[1,128]{1,0:T(1,128)S(1)}) custom-call(bf16[2,2,2,32,8192]{4,3,2,1,0:T(8,128)(2,1)} %bitcast.7, bf16[32,8192]{1,0:T(8,128)(2,1)} %bitcast.10, ...), custom_call_target="tpu_custom_call" | custom-call | tf_op jit(solution)/shard_map/pallas_call | solution.py:607
  28.7 1.5 %shard_map.103 = (bf16[32,8192]{1,0:T(8,128)(2,1)}, f32[32,8192]{1,0:T(8,128)}, f32[32,8192]{1,0:T(8,128)}, f32[8]{0:T(128)}) custom-call(bf16[32,8192]{1,0:T(8,128)(2,1)S(1)} %get-tuple-element.14.p_v, f32[32,8192]{1,0:T(8,128)S(1)} %get-tuple-element.15.upd, f32[32,8192]{1,0:T(8,128)S(1)} %get-tuple-element.16.new1_v, ...), custom_call_target="tpu_custom_call" | custom-call | tf_op jit(solution)/shard_map/pallas_call | solution.py:644
